TPU v7x, 128 devices: a whole 4x4x4 slice. The times are simulated.
128 devices in a mesh: ocn: 8 (over z, core), grp: 16 (over x, y).
Axes of the slice: x: 4, y: 4, z: 4, core: 2. Of those that a mesh axis runs over, the one named last changes fastest.
Arguments:
- tracers: float32 [2, 32, 512, 2048], P(None, None, 'grp', 'ocn'), may hold values from -6 to 6
- velocity: float32 [2, 32, 512, 2048], P(None, None, 'grp', 'ocn'), may hold values from -3 to 3
- remap_weights: bfloat16 [512, 8, 128, 128], P('grp'), may hold values from -0.25 to 0.25
- remap_blocks: int32 [512, 8], P('grp'), may hold values from 0 to 8191
- remap_count: int32 [512], P('grp'), may hold values from 1 to 8, as said below
- ice_velocity: float32 [2, 65536], P(None, 'grp'), may hold values from -3 to 3
- ice_mass_rate: float32 [65536], P('grp'), may hold values from 0.5 to 4
- ice_strength: float32 [65536], P('grp'), may hold values from 0.5 to 8
- wind_stress: float32 [2, 65536], P(None, 'grp'), may hold values from -6 to 6
Outputs:
- tracers_next: float32 [2, 32, 512, 2048], P(None, None, 'grp', 'ocn')
- surface_flux: float32 [3, 512, 2048], P(None, 'grp', 'ocn')
- ice_final: float32 [2, 65536], P(None, 'grp')
Inputs may be any that keep to these rules, and one draw needn't show every extreme that they name: `remap_count`: every ice block has at least one live entry. The ice blocks of the first and of the last index of grp have 7 or 8 live entries; all others have 1 or 2.
All inputs are finite; a program needn't handle non-finite values.
Results may differ from a plain program's by a relative error of at most 0.0006.
The roundings to bfloat16 on the way count: a program that leaves them out, or rounds other values in their place, can miss the bound.
Values may be sent and summed in bfloat16 or wider, within the bound.
A program may use at most 128 MiB of HBM per device.

v0:
```python
import functools

import jax
import jax.numpy as jnp
from jax import lax
from jax.sharding import Mesh
from jax.sharding import PartitionSpec as P

BS = 128
K = 8
ITERS = 4
DEPTH = 3
GRP = ("grp_0", "grp_1")


def sent_to_all(shard, axis):
    size = lax.axis_size(axis)
    return lax.all_to_all(
        jnp.broadcast_to(shard[None], (size, *shard.shape)), axis, 0, 0, tiled=True
    )


def in_order(parts, dim):
    dims = list(parts.shape[1:])
    dims[dim] *= parts.shape[0]
    return jnp.moveaxis(parts, 0, dim).reshape(dims)


def collect(shard, axis, dim):
    parts = sent_to_all(shard, axis)
    return in_order(parts, dim)


def taken_together(shard, axis):
    everything = sent_to_all(shard, axis)
    return jnp.sum(everything, axis=0)


def padded_2(block, sides, width):
    for axis, dim in sides:
        count = lax.axis_size(axis)
        forward = [(i, i + 1) for i in range(count - 1)]
        backward = [(target, source) for source, target in forward]
        low = lax.ppermute(
            lax.slice_in_dim(block, block.shape[dim] - width, None, axis=dim), axis, forward
        )
        high = lax.ppermute(lax.slice_in_dim(block, 0, width, axis=dim), axis, backward)
        block = jnp.concatenate([low, block, high], axis=dim)
    return block


def one_axis_at_a_time(shard, axes):
    return functools.reduce(lax.psum, axes, shard)


def on_device(
    tracers,
    velocity,
    remap_weights,
    remap_blocks,
    remap_count,
    ice_velocity,
    ice_mass_rate,
    ice_strength,
    wind_stress,
):
    n_grp = lax.axis_size(GRP)
    column = lax.axis_index("ocn")
    height = tracers.shape[2]
    across = tracers.shape[3]
    block_count = height * across // BS
    ice_blocks = remap_count.shape[0]
    entries = ice_blocks * K
    blocks_flat = remap_blocks.reshape(-1)
    valid = (jnp.arange(K)[None, :] < remap_count[:, None]).reshape(-1)
    owner_column = blocks_flat // (n_grp * block_count)
    local_rows = blocks_flat % (n_grp * block_count)
    mine = valid & (owner_column == column)
    weights = remap_weights.reshape(entries, BS, BS)
    surface = jnp.stack([tracers[0, 0], tracers[1, 0], velocity[0, 0], velocity[1, 0]]).astype(
        jnp.bfloat16
    )
    surface = surface.reshape(4, block_count, BS).transpose(1, 0, 2).reshape(block_count, 4 * BS)
    piece = collect(surface, GRP, 0)
    hits = (local_rows[:, None] == jnp.arange(piece.shape[0])[None, :]) & mine[:, None]
    chosen = jnp.dot(hits.astype(jnp.bfloat16), piece, preferred_element_type=jnp.float32)
    source = chosen.astype(jnp.bfloat16).reshape(entries, 4, BS)
    result = jnp.einsum("eij,efj->efi", weights, source, preferred_element_type=jnp.float32)
    remapped = taken_together(result.reshape(ice_blocks, K, 4, BS).sum(axis=1), "ocn")
    fields = remapped.transpose(1, 0, 2).reshape(4, ice_blocks * BS)
    ocean_current = fields[2:4]
    base = ice_mass_rate * ice_velocity + wind_stress + ocean_current
    total = 2.0 * ice_velocity.shape[1] * n_grp
    current = ice_velocity
    gvals = []
    fvals = []
    for step in range(ITERS):
        relax_padded = padded_2(current, ((GRP, 1),), 1)
        left = relax_padded[:, :-2]
        right = relax_padded[:, 2:]
        strain = 0.5 * (right - left)
        zeta = ice_strength / (2.0 * jnp.sqrt(jnp.sum(strain * strain, axis=0) + 0.25))
        gnew = (base + zeta * (left + right)) / (ice_mass_rate + 1.0 + 2.0 * zeta)
        gvals.append(gnew)
        fvals.append(gnew - current)
        if step == 0:
            current = gnew
            continue
        depth = min(step, DEPTH)
        diffs = jnp.stack([fvals[j] - fvals[j - 1] for j in range(step - depth + 1, step + 1)])
        gdiffs = jnp.stack([gvals[j] - gvals[j - 1] for j in range(step - depth + 1, step + 1)])
        gram_local = jnp.einsum("aij,bij->ab", diffs, diffs, precision=lax.Precision.HIGHEST)
        rhs_local = jnp.einsum("aij,ij->a", diffs, fvals[step], precision=lax.Precision.HIGHEST)
        gram_raw, rhs_raw = (
            one_axis_at_a_time(gram_local, GRP),
            one_axis_at_a_time(rhs_local, GRP),
        )
        norms = jnp.sqrt(jnp.diagonal(gram_raw) / total + 1e-06)
        gram = gram_raw / total / (norms[:, None] * norms[None, :])
        rhs = rhs_raw / total / norms
        factor = jnp.linalg.cholesky(gram + 0.1 * jnp.eye(depth, dtype=jnp.float32))
        coef = jax.scipy.linalg.cho_solve((factor, True), rhs)
        current = gnew - jnp.einsum(
            "a,aij->ij", coef / norms, gdiffs, precision=lax.Precision.HIGHEST
        )
    heat = 0.5 * (-0.05 * fields[1] - fields[0])
    ice_flux = jnp.concatenate([current - ocean_current, heat[None]], axis=0).astype(jnp.bfloat16)
    flux_blocks = ice_flux.reshape(3, ice_blocks, BS).transpose(1, 0, 2)
    flux_entries = jnp.broadcast_to(flux_blocks[:, None], (ice_blocks, K, 3, BS)).reshape(
        entries, 3, BS
    )
    contrib = jnp.einsum("eij,efi->efj", weights, flux_entries, preferred_element_type=jnp.float32)
    contrib = contrib.reshape(entries, 3 * BS)
    target = local_rows // block_count
    within = local_rows % block_count
    onehot = ((target[:, None] == jnp.arange(n_grp)[None, :]) & mine[:, None]).astype(jnp.int32)
    earlier = jnp.cumsum(onehot, axis=0) - onehot
    rank = jnp.sum(earlier * onehot, axis=1)
    slot = target * entries + rank
    select = (jnp.arange(n_grp * entries)[:, None] == slot[None, :]) & mine[None, :]
    packed = jnp.dot(select.astype(jnp.float32), contrib, precision=lax.Precision.HIGHEST)
    packed = packed.reshape(n_grp, entries, 3 * BS)
    labels = jnp.sum(select.astype(jnp.int32) * (within + 1)[None, :], axis=1) - 1
    labels = labels.reshape(n_grp, entries)
    arrived, arrived_labels = (
        lax.all_to_all(packed, GRP, split_axis=0, concat_axis=0, tiled=True),
        lax.all_to_all(labels, GRP, split_axis=0, concat_axis=0, tiled=True),
    )
    landing = (jnp.arange(block_count)[:, None] == arrived_labels.reshape(-1)[None, :]).astype(
        jnp.float32
    )
    returned = jnp.dot(landing, arrived.reshape(-1, 3 * BS), precision=lax.Precision.HIGHEST)
    surface_flux = (
        returned.reshape(block_count, 3, BS).transpose(1, 0, 2).reshape(3, height, across)
    )
    padded = padded_2(tracers, (("ocn", 3), (GRP, 2)), 1)
    padded = jnp.pad(padded, ((0, 0), (1, 1), (0, 0), (0, 0)))
    centre = padded[:, 1:-1, 1:-1, 1:-1]
    east = padded[:, 1:-1, 1:-1, 2:]
    west = padded[:, 1:-1, 1:-1, :-2]
    north = padded[:, 1:-1, 2:, 1:-1]
    south = padded[:, 1:-1, :-2, 1:-1]
    upper = padded[:, :-2, 1:-1, 1:-1]
    lower = padded[:, 2:, 1:-1, 1:-1]
    advect = velocity[0][None] * (east - west) * 0.5 + velocity[1][None] * (north - south) * 0.5
    tracers_next = (
        centre
        + 0.2 * (east + west + north + south - 4.0 * centre)
        - 0.5 * advect
        + 0.2 * (upper + lower - 2.0 * centre)
    )
    tracers_next = tracers_next.at[0, 0].add(0.5 * surface_flux[2])
    return (tracers_next, surface_flux, current)


def solution(mesh):
    finer = Mesh(mesh.devices.reshape(mesh.shape["ocn"], 4, 4), ("ocn", "grp_0", "grp_1"))
    placed = (
        P(None, None, GRP, "ocn"),
        P(None, None, GRP, "ocn"),
        P(GRP, None, None, None),
        P(GRP, None),
        P(GRP),
        P(None, GRP),
        P(GRP),
        P(GRP),
        P(None, GRP),
    )
    return jax.shard_map(
        on_device,
        mesh=finer,
        in_specs=placed,
        out_specs=(P(None, None, GRP, "ocn"), P(None, GRP, "ocn"), P(None, GRP)),
        check_vma=False,
    )
```

profile of v0, /device:TPU:2, one launch (start us, length us, event | category | flops | bytes accessed | tf_op | source)
XLA Modules:
  0.0 277.4 jit_solution(15324827232844272759)
XLA Ops:
  0.6 1.9 convert.23
  3.3 1.1 broadcast_in_dim.18
  4.4 7.5 %all-to-all-start.1 = ((bf16[16,64,512]{2,1,0:T(8,128)(2,1)}), bf16[16,64,512]{2,1,0:T(8,128)(2,1)S(1)}, u32[]{:S(2)}, u32[]{:S(2)}) async-start(bf16[16,64,512]{2,1,0:T(8,128)(2,1)} %broadcast_in_dim.18), calls=%async_computation.1 | async-start | bytes 2097152 | tf_op jit(solution)/shard_map/all_to_all | solution.py:18
  11.9 4.6 %collective-permute-start.4 = (f32[2,1]{1,0:T(2,128)S(1)}, f32[2,1]{1,0:T(2,128)S(1)}, u32[]{:S(2)}, u32[]{:S(2)}) collective-permute-start(f32[2,1]{1,0:T(2,128)S(1)} %get-tuple-element.80), channel_id=1, source_target_pairs={{1,0},{2,1},{3,2},{4,3},{5,4},{6,5},{7,6},{8,7},{9,8},{10,9},{11,1... | collective-permute-start | bytes 32 | tf_op jit(solution)/shard_map/ppermute | solution.py:47
  16.5 1.9 collective-permute-start.5
  20.3 6.6 %all-to-all-done.1 = bf16[16,64,512]{2,1,0:T(8,128)(2,1)S(1)} async-done(((bf16[16,64,512]{2,1,0:T(8,128)(2,1)}), bf16[16,64,512]{2,1,0:T(8,128)(2,1)S(1)}, u32[]{:S(2)}, u32[]{:S(2)}) %all-to-all-start.1) | async-done | bytes 1048608 | tf_op jit(solution)/shard_map/all_to_all | solution.py:18
  27.5 7.8 %bitcast_reduce_fusion = f32[32,4,128]{2,1,0:T(4,128)S(1)} fusion(bf16[256,4,128]{2,1,0:T(4,128)(2,1)S(1)} %reshape.477, bf16[256,128,128]{2,1,0:T(8,128)(2,1)} %bitcast.170), kind=kOutput, calls=%fused_computation.50 | convolution fusion | flops 33669120 | bytes 8716288 | tf_op jit(solution)/shard_map/eij,efj->efi/dot_general | solution.py:88
  36.2 5.3 %all-to-all-start.2 = ((f32[8,32,4,128]{3,1,2,0:T(8,128)}), f32[8,32,4,128]{3,1,2,0:T(8,128)S(1)}, u32[]{:S(2)}, u32[]{:S(2)}) async-start(f32[8,32,4,128]{3,1,2,0:T(8,128)} %broadcast_in_dim.19), calls=%async_computation.2 | async-start | bytes 1048576 | tf_op jit(solution)/shard_map/all_to_all | solution.py:18
  41.8 10.1 %all-to-all-done.2 = f32[8,32,4,128]{3,1,2,0:T(8,128)S(1)} async-done(((f32[8,32,4,128]{3,1,2,0:T(8,128)}), f32[8,32,4,128]{3,1,2,0:T(8,128)S(1)}, u32[]{:S(2)}, u32[]{:S(2)}) %all-to-all-start.2) | async-done | bytes 524320 | tf_op jit(solution)/shard_map/all_to_all | solution.py:18
  52.1 4.3 %collective-permute-start.6 = (f32[2,1]{1,0:T(2,128)S(1)}, f32[2,1]{1,0:T(2,128)S(1)}, u32[]{:S(2)}, u32[]{:S(2)}) collective-permute-start(f32[2,1]{1,0:T(2,128)S(1)} %get-tuple-element.78), channel_id=1, source_target_pairs={{1,0},{2,1},{3,2},{4,3},{5,4},{6,5},{7,6},{8,7},{9,8},{10,9},{11,1... | collective-permute-start | bytes 32 | tf_op jit(solution)/shard_map/ppermute | solution.py:47
  56.4 1.9 collective-permute-start.7
  58.4 5.6 %collective-permute-done.7 = f32[2,1]{1,0:T(2,128)S(1)} collective-permute-done((f32[2,1]{1,0:T(2,128)S(1)}, f32[2,1]{1,0:T(2,128)S(1)}, u32[]{:S(2)}, u32[]{:S(2)}) %collective-permute-start.7) | collective-permute-done | bytes 40 | tf_op jit(solution)/shard_map/ppermute | solution.py:44
  64.9 8.2 %all-reduce.6 = (f32[1]{0:T(128)}, f32[1,1]{1,0:T(1,128)}) all-reduce(f32[1]{0:T(128)} %bitcast.11, f32[1,1]{1,0:T(1,128)} %bitcast.12), channel_id=1, replica_groups=mesh['ocn'=8,'grp_0'=4,'grp_1'=4] {'grp_0'}, use_global_device_ids=true, to_apply=%region_8.9 | all-reduce | flops 2 | bytes 16 | tf_op jit(solution)/shard_map/psum | solution.py:53
  73.1 8.8 %all-reduce.3 = (f32[1]{0:T(128)}, f32[1,1]{1,0:T(1,128)}) all-reduce(f32[1]{0:T(128)} %get-tuple-element.36, f32[1,1]{1,0:T(1,128)} %get-tuple-element.37), channel_id=1, replica_groups=mesh['ocn'=8,'grp_0'=4,'grp_1'=4] {'grp_1'}, use_global_device_ids=true, to_apply=%region_9.10 | all-reduce | flops 2 | bytes 16 | tf_op jit(solution)/shard_map/psum | solution.py:53
  83.6 5.3 %collective-permute-start.8 = (f32[2,1]{1,0:T(2,128)S(1)}, f32[2,1]{1,0:T(2,128)S(1)}, u32[]{:S(2)}, u32[]{:S(2)}) collective-permute-start(f32[2,1]{1,0:T(2,128)S(1)} %get-tuple-element.76), channel_id=1, source_target_pairs={{1,0},{2,1},{3,2},{4,3},{5,4},{6,5},{7,6},{8,7},{9,8},{10,9},{11,1... | collective-permute-start | bytes 32 | tf_op jit(solution)/shard_map/ppermute | solution.py:47
  88.9 1.9 collective-permute-start.9
  90.9 5.6 %collective-permute-done.9 = f32[2,1]{1,0:T(2,128)S(1)} collective-permute-done((f32[2,1]{1,0:T(2,128)S(1)}, f32[2,1]{1,0:T(2,128)S(1)}, u32[]{:S(2)}, u32[]{:S(2)}) %collective-permute-start.9) | collective-permute-done | bytes 40 | tf_op jit(solution)/shard_map/ppermute | solution.py:44
  98.2 6.7 %all-reduce.5 = (f32[2,2]{0,1:T(2,128)S(1)}, f32[2]{0:T(128)S(1)}) all-reduce(f32[2,2]{0,1:T(2,128)S(1)} %convolution_bitcast_fusion.2, f32[2]{0:T(128)S(1)} %convolution_bitcast_fusion.8), channel_id=1, replica_groups=mesh['ocn'=8,'grp_0'=4,'grp_1'=4] {'grp_0'}, use_global_device_ids=true, to_apply=%region_13.14 | all-reduce | flops 6 | bytes 48 | tf_op jit(solution)/shard_map/psum | solution.py:53
  105.0 9.0 %all-reduce.2 = (f32[2,2]{0,1:T(2,128)S(1)}, f32[2]{0:T(128)S(1)}) all-reduce(f32[2,2]{0,1:T(2,128)S(1)} %get-tuple-element.34, f32[2]{0:T(128)S(1)} %get-tuple-element.35), channel_id=1, replica_groups=mesh['ocn'=8,'grp_0'=4,'grp_1'=4] {'grp_1'}, use_global_device_ids=true, to_apply=%region_14.15 | all-reduce | flops 6 | bytes 48 | tf_op jit(solution)/shard_map/psum | solution.py:53
  117.7 5.1 %collective-permute-start.10 = (f32[2,1]{1,0:T(2,128)S(1)}, f32[2,1]{1,0:T(2,128)S(1)}, u32[]{:S(2)}, u32[]{:S(2)}) collective-permute-start(f32[2,1]{1,0:T(2,128)S(1)} %get-tuple-element.74), channel_id=1, source_target_pairs={{1,0},{2,1},{3,2},{4,3},{5,4},{6,5},{7,6},{8,7},{9,8},{10,9},{11,1... | collective-permute-start | bytes 32 | tf_op jit(solution)/shard_map/ppermute | solution.py:47
  122.8 1.9 collective-permute-start.11
  124.7 5.6 %collective-permute-done.11 = f32[2,1]{1,0:T(2,128)S(1)} collective-permute-done((f32[2,1]{1,0:T(2,128)S(1)}, f32[2,1]{1,0:T(2,128)S(1)}, u32[]{:S(2)}, u32[]{:S(2)}) %collective-permute-start.11) | collective-permute-done | bytes 40 | tf_op jit(solution)/shard_map/ppermute | solution.py:44
  132.2 6.5 %all-reduce.4 = (f32[3,3]{0,1:T(4,128)S(1)}, f32[3]{0:T(128)S(1)}) all-reduce(f32[3,3]{0,1:T(4,128)S(1)} %convolution_bitcast_fusion.1, f32[3]{0:T(128)S(1)} %convolution_bitcast_fusion.5), channel_id=1, replica_groups=mesh['ocn'=8,'grp_0'=4,'grp_1'=4] {'grp_0'}, use_global_device_ids=true, to_apply=%region_20.21 | all-reduce | flops 12 | bytes 96 | tf_op jit(solution)/shard_map/psum | solution.py:53
  138.8 9.4 %all-reduce.1 = (f32[3,3]{0,1:T(4,128)S(1)}, f32[3]{0:T(128)S(1)}) all-reduce(f32[3,3]{0,1:T(4,128)S(1)} %get-tuple-element.32, f32[3]{0:T(128)S(1)} %get-tuple-element.33), channel_id=1, replica_groups=mesh['ocn'=8,'grp_0'=4,'grp_1'=4] {'grp_1'}, use_global_device_ids=true, to_apply=%region_21.22 | all-reduce | flops 12 | bytes 96 | tf_op jit(solution)/shard_map/psum | solution.py:53
  152.7 5.6 %fusion.64 = f32[256,3,128]{2,1,0:T(4,128)S(1)} fusion(bf16[256,3,128]{2,1,0:T(4,128)(2,1)S(1)} %bitcast.174, bf16[256,128,128]{2,1,0:T(8,128)(2,1)} %bitcast.171), kind=kOutput, calls=%fused_computation.202 | convolution fusion | flops 25165824 | bytes 8978432 | tf_op jit(solution)/shard_map/eij,efi->efj/dot_general | solution.py:132
  158.6 5.4 %fusion.1 = f32[16,256,384]{2,1,0:T(8,128)} fusion(f32[256,384,1]{0,1,2:T(8,128)S(1)} %bitcast.173, s32[256]{0:T(256)S(1)} %multiply_add_fusion.5, s32[16,256]{1,0:T(8,128)S(1)} %multiply_add_fusion.4, pred[256]{0:T(512)(128)(4,1)S(1)} %compare_and_fusion.1), kind=kOutput, calls=%fused_computation.7 | convolution fusion | flops 4833935360 | bytes 6702336 | tf_op jit(solution)/shard_map/dot_general | solution.py:141
  164.0 6.3 %all-to-all-start.3 = ((f32[16,256,384]{2,1,0:T(8,128)}), f32[16,256,384]{2,1,0:T(8,128)}, u32[]{:S(2)}, u32[]{:S(2)}) async-start(f32[16,256,384]{2,1,0:T(8,128)} %fusion.1), calls=%async_computation.3 | async-start | bytes 12582912 | tf_op jit(solution)/shard_map/all_to_all | solution.py:146
  170.3 1.3 fusion.57
  171.6 1.8 copy.196
  173.4 1.3 collective-permute-start
  175.2 3.2 %collective-permute-start.1 = (f32[2,32,32,1]{2,1,3,0:T(8,128)S(1)}, f32[2,32,32,1]{2,1,3,0:T(8,128)S(1)}, u32[]{:S(2)}, u32[]{:S(2)}) collective-permute-start(f32[2,32,32,1]{2,1,3,0:T(8,128)S(1)} %copy.197), channel_id=1, source_target_pairs={{0,16},{16,32},{32,48},{48,64},{64,80},{80,96},{96,112},{1,17},{17... | collective-permute-start | bytes 24584 | tf_op jit(solution)/shard_map/ppermute | solution.py:44
  178.3 1.5 slice_bitcast_fusion.1
  179.9 1.0 select_reduce_fusion
  180.8 1.2 copy.145
  182.1 1.0 copy.137
  183.1 1.8 copy.139
  184.9 1.0 pad_maximum_fusion.9
  185.9 4.7 %collective-permute-start.2 = (f32[2,32,1,258]{3,1,2,0:T(8,128)S(1)}, f32[2,32,1,258]{3,1,2,0:T(8,128)S(1)}, u32[]{:S(2)}, u32[]{:S(2)}) collective-permute-start(f32[2,32,1,258]{3,1,2,0:T(8,128)S(1)} %get-tuple-element.62), channel_id=1, source_target_pairs={{1,0},{2,1},{3,2},{4,3},{5,4},{6,5},{7,6},{8,7},{9,8},{10,9},{11,1... | collective-permute-start | bytes 198152 | tf_op jit(solution)/shard_map/ppermute | solution.py:47
  190.6 1.9 collective-permute-start.3
  193.2 1.6 copy.146
  194.8 1.6 copy.147
  196.4 41.3 %collective-permute-done.2 = f32[2,32,1,258]{3,1,2,0:T(8,128)S(1)} collective-permute-done((f32[2,32,1,258]{3,1,2,0:T(8,128)S(1)}, f32[2,32,1,258]{3,1,2,0:T(8,128)S(1)}, u32[]{:S(2)}, u32[]{:S(2)}) %collective-permute-start.2) | collective-permute-done | bytes 66080 | tf_op jit(solution)/shard_map/ppermute | solution.py:47
  237.7 3.3 %select_maximum_fusion = f32[2,34,34,258]{3,1,2,0:T(8,128)} fusion(f32[2,32,1,258]{3,1,2,0:T(8,128)S(1)} %collective-permute-done.2, f32[2,32,1,258]{3,1,2,0:T(8,128)S(1)} %collective-permute-done.3, f32[2,32,32,1]{3,1,2,0:T(8,128)S(1)} %copy.137, f32[2,32,32,256]{3,1,2,0:T(8,128)S(1)} %copy.145, f32[2,32,32,1]{3,1,2,0:T(8,128)S(1)} %copy-done.2), kind=kLoop, calls=%fused_computation.10 | loop fusion | flops 7157952 | bytes 4631616 | tf_op jit(solution)/shard_map/concatenate | solution.py:48
  241.0 12.2 %all-to-all-start = ((s32[16,1,256]{2,1,0:T(1,128)}), s32[16,1,256]{2,1,0:T(1,128)S(1)}, u32[]{:S(2)}, u32[]{:S(2)}) async-start(s32[16,1,256]{2,1,0:T(1,128)} %bitcast.3), calls=%async_computation | async-start | bytes 32768 | tf_op jit(solution)/shard_map/all_to_all | solution.py:147
  253.2 7.9 %fusion.7 = f32[2,32,32,256]{3,1,2,0:T(8,128)} fusion(f32[2,34,34,258]{3,1,2,0:T(8,128)} %select_maximum_fusion, f32[2,32,32,256]{3,1,2,0:T(8,128)S(1)} %copy.145, f32[2,32,32,1]{3,1,2,0:T(8,128)S(1)} %copy.137, f32[2,32,32,1]{3,1,2,0:T(8,128)} %copy.139, f32[2,32,1,258]{3,1,2,0:T(8,128)S(1)} %collective-permute-done.3, ...), kind=kLoop, calls=%fused_computation.18 | loop fusion | flops 14155776 | bytes 10634240 | tf_op jit(solution)/shard_map/add | solution.py:167
  261.1 6.6 %copy.174 = f32[384,4096]{1,0:T(8,128)} copy(f32[384,4096]{0,1:T(8,128)} %bitcast.53) | data formatting | bytes 12582912 | tf_op jit(solution)/shard_map/dot_general | solution.py:152
  267.7 6.3 %convolution_bitcast_fusion = f32[3,64,128]{2,1,0:T(8,128)S(1)} fusion(f32[3,128,4096]{2,1,0:T(8,128)} %bitcast.172, s32[4096]{0:T(1024)S(1)} %bitcast.185), kind=kOutput, calls=%fused_computation.31 | convolution fusion | flops 1208221696 | bytes 6406144 | tf_op jit(solution)/shard_map/dot_general | solution.py:152
  274.9 2.5 copy.176
  (150 shorter events, 19.3 us)
Async XLA Ops:
  0.6 2.2 copy-start.4
  3.0 8.8 %copy-start.9 = (f32[2,4096]{1,0:T(2,128)S(1)}, f32[2,4096]{1,0:T(2,128)}, u32[]{:S(2)}) copy-start(f32[2,4096]{1,0:T(2,128)} %param.16) | copy-start | bytes 98308
  3.0 15.4 %copy-start.12 = (s32[32,8]{0,1:T(8,128)S(1)}, s32[32,8]{0,1:T(8,128)}, u32[]{:S(2)}) copy-start(s32[32,8]{0,1:T(8,128)} %param.14) | copy-start | bytes 3076
  3.0 15.7 %copy-start.13 = (s32[32]{0:T(128)S(1)}, s32[32]{0:T(128)}, u32[]{:S(2)}) copy-start(s32[32]{0:T(128)} %param.15) | copy-start | bytes 388
  4.4 22.5 %all-to-all-start.1 = ((bf16[16,64,512]{2,1,0:T(8,128)(2,1)}), bf16[16,64,512]{2,1,0:T(8,128)(2,1)S(1)}, u32[]{:S(2)}, u32[]{:S(2)}) async-start(bf16[16,64,512]{2,1,0:T(8,128)(2,1)} %broadcast_in_dim.18), calls=%async_computation.1 | async-start | bytes 2097152 | tf_op jit(solution)/shard_map/all_to_all | solution.py:18
  11.9 29.6 %collective-permute-start.4 = (f32[2,1]{1,0:T(2,128)S(1)}, f32[2,1]{1,0:T(2,128)S(1)}, u32[]{:S(2)}, u32[]{:S(2)}) collective-permute-start(f32[2,1]{1,0:T(2,128)S(1)} %get-tuple-element.80), channel_id=1, source_target_pairs={{1,0},{2,1},{3,2},{4,3},{5,4},{6,5},{7,6},{8,7},{9,8},{10,9},{11,1... | collective-permute-start | bytes 32 | tf_op jit(solution)/shard_map/ppermute | solution.py:47
  16.5 25.1 %collective-permute-start.5 = (f32[2,1]{1,0:T(2,128)S(1)}, f32[2,1]{1,0:T(2,128)S(1)}, u32[]{:S(2)}, u32[]{:S(2)}) collective-permute-start(f32[2,1]{1,0:T(2,128)S(1)} %get-tuple-element.79), channel_id=1, source_target_pairs={{0,1},{1,2},{2,3},{3,4},{4,5},{5,6},{6,7},{7,8},{8,9},{9,10},{10,1... | collective-permute-start | bytes 32 | tf_op jit(solution)/shard_map/ppermute | solution.py:44
  27.5 14.3 %copy-start.8 = (f32[4096]{0:T(1024)S(1)}, f32[4096]{0:T(1024)}, u32[]{:S(2)}) copy-start(f32[4096]{0:T(1024)} %param.17) | copy-start | bytes 49156
  27.5 14.3 %copy-start.10 = (f32[4096]{0:T(1024)S(1)}, f32[4096]{0:T(1024)}, u32[]{:S(2)}) copy-start(f32[4096]{0:T(1024)} %param.18) | copy-start | bytes 49156
  35.3 16.6 %copy-start.11 = (f32[2,4096]{1,0:T(2,128)S(1)}, f32[2,4096]{1,0:T(2,128)}, u32[]{:S(2)}) copy-start(f32[2,4096]{1,0:T(2,128)} %param.19) | copy-start | bytes 98308
  36.2 15.6 %all-to-all-start.2 = ((f32[8,32,4,128]{3,1,2,0:T(8,128)}), f32[8,32,4,128]{3,1,2,0:T(8,128)S(1)}, u32[]{:S(2)}, u32[]{:S(2)}) async-start(f32[8,32,4,128]{3,1,2,0:T(8,128)} %broadcast_in_dim.19), calls=%async_computation.2 | async-start | bytes 1048576 | tf_op jit(solution)/shard_map/all_to_all | solution.py:18
  52.1 6.2 %collective-permute-start.6 = (f32[2,1]{1,0:T(2,128)S(1)}, f32[2,1]{1,0:T(2,128)S(1)}, u32[]{:S(2)}, u32[]{:S(2)}) collective-permute-start(f32[2,1]{1,0:T(2,128)S(1)} %get-tuple-element.78), channel_id=1, source_target_pairs={{1,0},{2,1},{3,2},{4,3},{5,4},{6,5},{7,6},{8,7},{9,8},{10,9},{11,1... | collective-permute-start | bytes 32 | tf_op jit(solution)/shard_map/ppermute | solution.py:47
  56.4 7.6 %collective-permute-start.7 = (f32[2,1]{1,0:T(2,128)S(1)}, f32[2,1]{1,0:T(2,128)S(1)}, u32[]{:S(2)}, u32[]{:S(2)}) collective-permute-start(f32[2,1]{1,0:T(2,128)S(1)} %get-tuple-element.77), channel_id=1, source_target_pairs={{0,1},{1,2},{2,3},{3,4},{4,5},{5,6},{6,7},{7,8},{8,9},{9,10},{10,1... | collective-permute-start | bytes 32 | tf_op jit(solution)/shard_map/ppermute | solution.py:44
  83.6 7.3 %collective-permute-start.8 = (f32[2,1]{1,0:T(2,128)S(1)}, f32[2,1]{1,0:T(2,128)S(1)}, u32[]{:S(2)}, u32[]{:S(2)}) collective-permute-start(f32[2,1]{1,0:T(2,128)S(1)} %get-tuple-element.76), channel_id=1, source_target_pairs={{1,0},{2,1},{3,2},{4,3},{5,4},{6,5},{7,6},{8,7},{9,8},{10,9},{11,1... | collective-permute-start | bytes 32 | tf_op jit(solution)/shard_map/ppermute | solution.py:47
  88.9 7.6 %collective-permute-start.9 = (f32[2,1]{1,0:T(2,128)S(1)}, f32[2,1]{1,0:T(2,128)S(1)}, u32[]{:S(2)}, u32[]{:S(2)}) collective-permute-start(f32[2,1]{1,0:T(2,128)S(1)} %get-tuple-element.75), channel_id=1, source_target_pairs={{0,1},{1,2},{2,3},{3,4},{4,5},{5,6},{6,7},{7,8},{8,9},{9,10},{10,1... | collective-permute-start | bytes 32 | tf_op jit(solution)/shard_map/ppermute | solution.py:44
  117.7 7.0 %collective-permute-start.10 = (f32[2,1]{1,0:T(2,128)S(1)}, f32[2,1]{1,0:T(2,128)S(1)}, u32[]{:S(2)}, u32[]{:S(2)}) collective-permute-start(f32[2,1]{1,0:T(2,128)S(1)} %get-tuple-element.74), channel_id=1, source_target_pairs={{1,0},{2,1},{3,2},{4,3},{5,4},{6,5},{7,6},{8,7},{9,8},{10,9},{11,1... | collective-permute-start | bytes 32 | tf_op jit(solution)/shard_map/ppermute | solution.py:47
  122.8 7.6 %collective-permute-start.11 = (f32[2,1]{1,0:T(2,128)S(1)}, f32[2,1]{1,0:T(2,128)S(1)}, u32[]{:S(2)}, u32[]{:S(2)}) collective-permute-start(f32[2,1]{1,0:T(2,128)S(1)} %get-tuple-element.73), channel_id=1, source_target_pairs={{0,1},{1,2},{2,3},{3,4},{4,5},{5,6},{6,7},{7,8},{8,9},{9,10},{10,1... | collective-permute-start | bytes 32 | tf_op jit(solution)/shard_map/ppermute | solution.py:44
  164.0 6.3 %copy-start = (f32[2,32,32,256]{3,2,1,0:T(8,128)S(1)}, f32[2,32,32,256]{3,2,1,0:T(8,128)}, u32[]{:S(2)}) copy-start(f32[2,32,32,256]{3,2,1,0:T(8,128)} %param.11) | copy-start | bytes 6291460
  164.0 77.0 %all-to-all-start.3 = ((f32[16,256,384]{2,1,0:T(8,128)}), f32[16,256,384]{2,1,0:T(8,128)}, u32[]{:S(2)}, u32[]{:S(2)}) async-start(f32[16,256,384]{2,1,0:T(8,128)} %fusion.1), calls=%async_computation.3 | async-start | bytes 12582912 | tf_op jit(solution)/shard_map/all_to_all | solution.py:146
  171.6 6.7 %copy-start.5 = (f32[2,32,32,256]{3,2,1,0:T(8,128)S(1)}, f32[2,32,32,256]{3,2,1,0:T(8,128)}, u32[]{:S(2)}) copy-start(f32[2,32,32,256]{3,2,1,0:T(8,128)} %param.12) | copy-start | bytes 6291460
  173.4 8.7 %collective-permute-start = (f32[2,32,32,1]{2,1,3,0:T(8,128)S(1)}, f32[2,32,32,1]{2,1,3,0:T(8,128)S(1)}, u32[]{:S(2)}, u32[]{:S(2)}) collective-permute-start(f32[2,32,32,1]{2,1,3,0:T(8,128)S(1)} %copy.196), channel_id=1, source_target_pairs={{16,0},{32,16},{48,32},{64,48},{80,64},{96,80},{112,96},{17,1},{33... | collective-permute-start | bytes 24584 | tf_op jit(solution)/shard_map/ppermute | solution.py:47
  175.2 5.7 %copy-start.1 = (f32[2,32,32,256]{3,2,1,0:T(8,128)S(1)}, f32[2,32,32,256]{3,2,1,0:T(8,128)}, u32[]{:S(2)}) copy-start(f32[2,32,32,256]{3,2,1,0:T(8,128)} %param.11) | copy-start | bytes 6291460
  175.2 7.9 %collective-permute-start.1 = (f32[2,32,32,1]{2,1,3,0:T(8,128)S(1)}, f32[2,32,32,1]{2,1,3,0:T(8,128)S(1)}, u32[]{:S(2)}, u32[]{:S(2)}) collective-permute-start(f32[2,32,32,1]{2,1,3,0:T(8,128)S(1)} %copy.197), channel_id=1, source_target_pairs={{0,16},{16,32},{32,48},{48,64},{64,80},{80,96},{96,112},{1,17},{17... | collective-permute-start | bytes 24584 | tf_op jit(solution)/shard_map/ppermute | solution.py:44
  184.9 8.3 %copy-start.7 = (f32[32,32,256]{2,1,0:T(8,128)S(1)}, f32[32,32,256]{2,1,0:T(8,128)}, u32[]{:S(2)}) copy-start(f32[32,32,256]{2,1,0:T(8,128)} %get-tuple-element.63) | copy-start | bytes 3145732
  185.9 8.9 %copy-start.6 = (f32[32,32,256]{2,1,0:T(8,128)S(1)}, f32[32,32,256]{2,1,0:T(8,128)}, u32[]{:S(2)}) copy-start(f32[32,32,256]{2,1,0:T(8,128)} %get-tuple-element.64) | copy-start | bytes 3145732
  185.9 51.8 %collective-permute-start.2 = (f32[2,32,1,258]{3,1,2,0:T(8,128)S(1)}, f32[2,32,1,258]{3,1,2,0:T(8,128)S(1)}, u32[]{:S(2)}, u32[]{:S(2)}) collective-permute-start(f32[2,32,1,258]{3,1,2,0:T(8,128)S(1)} %get-tuple-element.62), channel_id=1, source_target_pairs={{1,0},{2,1},{3,2},{4,3},{5,4},{6,5},{7,6},{8,7},{9,8},{10,9},{11,1... | collective-permute-start | bytes 198152 | tf_op jit(solution)/shard_map/ppermute | solution.py:47
  190.6 47.1 %collective-permute-start.3 = (f32[2,32,1,258]{3,1,2,0:T(8,128)S(1)}, f32[2,32,1,258]{3,1,2,0:T(8,128)S(1)}, u32[]{:S(2)}, u32[]{:S(2)}) collective-permute-start(f32[2,32,1,258]{3,1,2,0:T(8,128)S(1)} %get-tuple-element.61), channel_id=1, source_target_pairs={{0,1},{1,2},{2,3},{3,4},{4,5},{5,6},{6,7},{7,8},{8,9},{9,10},{10,1... | collective-permute-start | bytes 198152 | tf_op jit(solution)/shard_map/ppermute | solution.py:44
  193.2 44.6 %copy-start.2 = (f32[2,32,32,1]{3,1,2,0:T(8,128)S(1)}, f32[2,32,32,1]{3,1,2,0:T(8,128)}, u32[]{:S(2)}) copy-start(f32[2,32,32,1]{3,1,2,0:T(8,128)} %copy.139) | copy-start | bytes 24580
  241.0 26.7 %all-to-all-start = ((s32[16,1,256]{2,1,0:T(1,128)}), s32[16,1,256]{2,1,0:T(1,128)S(1)}, u32[]{:S(2)}, u32[]{:S(2)}) async-start(s32[16,1,256]{2,1,0:T(1,128)} %bitcast.3), calls=%async_computation | async-start | bytes 32768 | tf_op jit(solution)/shard_map/all_to_all | solution.py:147
  267.7 7.0 %copy-start.3 = (f32[2,32,32,256]{3,1,2,0:T(8,128)S(1)}, f32[2,32,32,256]{3,1,2,0:T(8,128)}, u32[]{:S(2)}) copy-start(f32[2,32,32,256]{3,1,2,0:T(8,128)} %fusion.7) | copy-start | bytes 6291460
where the time goes:
time: 278 us; the launch traced here: 277 us
  waiting for transfers between devices  74.9 us (27%)
  starting transfers between devices  69.2 us (25%)
  blocking collectives  48.7 us (18%)
  matrix products  29.7 us (11%)
  local copies, waits for them, and re-layouts  28.1 us (10%)
  other arithmetic  23.8 us (9%)
  between operations  2.91 us (1%)
    psum x6, blocking collectives, one_axis_at_a_time(): return functools.reduce(lax.psum, axes, shard)  48.7 us
    ppermute x6, waiting for transfers between devices, padded_2(): lax.ppermute(lax.slice_in_dim(block, 0, width, axis=dim), axis, backward)  41.3 us
    ppermute x6, starting transfers between devices, padded_2(): lax.ppermute(lax.slice_in_dim(block, 0, width, axis=dim), axis, backward)  25.2 us
    ppermute x6, waiting for transfers between devices, padded_2(): lax.ppermute(lax.slice_in_dim(block, block.shape[dim] - width, None, axis...  16.9 us
    all_to_all x2, waiting for transfers between devices, sent_to_all(): lax.all_to_all(jnp.broadcast_to(shard[None], (size, *shard.shape)), axis,...  16.7 us
    all_to_all x2, starting transfers between devices, sent_to_all(): lax.all_to_all(jnp.broadcast_to(shard[None], (size, *shard.shape)), axis,...  12.8 us
    ppermute x6, starting transfers between devices, padded_2(): lax.ppermute(lax.slice_in_dim(block, block.shape[dim] - width, None, axis...  12.8 us
    all_to_all x1, starting transfers between devices, on_device(): lax.all_to_all(labels, GRP, split_axis=0, concat_axis=0, tiled=True)  12.2 us
  transfers between devices with their start and end apart: 16, of which 6 were waited for; matrix products, arithmetic and copies ran while one was open for 16% of the time, Pallas kernels for 0%

commit v1 on v0

v1 whole, which is shorter than its diff:
```python
import functools

import jax
import jax.numpy as jnp
from jax import lax
from jax.experimental import pallas as pl
from jax.experimental.pallas import tpu as pltpu
from jax.sharding import PartitionSpec as P

MESH = pl.DeviceIdType.MESH
F32 = jnp.float32
BF16 = jnp.bfloat16
N_OCN = 8
N_GRP = 16
N_ALL = N_OCN * N_GRP
LAST = N_GRP - 1
L = 32
CHUNKS = 22
PADDED = 32
ITERS = 4


def chunk_of(g):
    return 0 if g == 0 else (CHUNKS - 4 if g == LAST else 3 + g)


def chunks_of(g):
    return 4 if g in (0, LAST) else 1


def landed(ref, sem):
    pltpu.make_async_copy(ref, ref, sem).wait()


def kernel(
    tracers,
    velocity,
    weights,
    blocks,
    counts,
    u_in,
    wind,
    mass,
    strength,
    pre,
    flux,
    ice,
    t_v,
    v_v,
    w_v,
    level0,
    surf,
    codes,
    hits,
    hits_t,
    sel,
    slots_in,
    xs,
    q,
    hx_s,
    hx_r,
    hy_s,
    hy_r,
    u_pad,
    m_r,
    st_r,
    m2,
    st2,
    base,
    gval,
    fval,
    dval,
    fx,
    cbuf,
    crecv,
    dense,
    dense_in,
    local_sem,
    send_sem,
    recv_sem,
    halo_send,
    halo_recv,
):
    o = lax.axis_index("ocn")
    g = lax.axis_index("grp")
    first, last = g == 0, g == LAST
    polar = jnp.logical_or(first, last)
    inner = jnp.logical_and(g > 0, g < LAST)

    def send(src, dst, phase, ocn, grp):
        pltpu.make_async_remote_copy(
            src_ref=src,
            dst_ref=dst,
            send_sem=send_sem.at[phase],
            recv_sem=recv_sem.at[phase],
            device_id={"ocn": ocn, "grp": grp},
            device_id_type=MESH,
        ).start()

    def over_grp(src, dst, phase):
        for i in range(1, N_GRP):
            send(src, dst, phase, o, lax.rem(g + i, N_GRP))

    small = [
        pltpu.make_async_copy(tracers.at[0, 0], level0.at[0], local_sem.at[0]),
        pltpu.make_async_copy(tracers.at[1, 0], level0.at[1], local_sem.at[1]),
        pltpu.make_async_copy(velocity.at[0, 0], level0.at[2], local_sem.at[2]),
        pltpu.make_async_copy(velocity.at[1, 0], level0.at[3], local_sem.at[3]),
    ]
    for copy in small:
        copy.start()
    t_copy = pltpu.make_async_copy(tracers, t_v, local_sem.at[4])
    v_copy = pltpu.make_async_copy(velocity, v_v, local_sem.at[5])
    w_copy = pltpu.make_async_copy(weights.at[pl.ds(4 * o, 4)], w_v, local_sem.at[6])
    t_copy.start()
    w_copy.start()
    v_copy.start()

    barrier = pltpu.get_barrier_semaphore()
    for i in range(1, N_GRP):
        pl.semaphore_signal(
            barrier, inc=1, device_id={"ocn": o, "grp": lax.rem(g + i, N_GRP)}, device_id_type=MESH
        )
    for i in range(1, N_OCN):
        pl.semaphore_signal(
            barrier, inc=1, device_id={"ocn": lax.rem(o + i, N_OCN), "grp": g}, device_id_type=MESH
        )

    def fill_codes(at, count):
        for k in range(2 * count):
            for r in range(4):
                block = blocks[4 * o + r, k]
                code = jnp.where(k < counts[4 * o + r], block, -1)
                codes[at + k // 2, pl.ds((k % 2) * 4 + r, 1), :] = jnp.full((1, 128), code, jnp.int32)

    @pl.when(first)
    def _():
        fill_codes(0, 4)

    @pl.when(last)
    def _():
        fill_codes(CHUNKS - 4, 4)

    @pl.when(inner)
    def _():
        fill_codes(3 + g, 1)

    codes[pl.ds(CHUNKS, PADDED - CHUNKS)] = jnp.full((PADDED - CHUNKS, 8, 128), -1, jnp.int32)
    crecv[pl.ds(CHUNKS, PADDED - CHUNKS)] = jnp.zeros((PADDED - CHUNKS, 24, 128), F32)
    u_pad[0] = jnp.zeros((8, 128), F32)
    u_pad[N_ALL + 1] = jnp.zeros((8, 128), F32)
    u_pad[pl.ds(1 + 8 * g, 8)] = u_in[...]
    m_r[pl.ds(8 * g, 8)] = mass[...]
    st_r[pl.ds(8 * g, 8)] = strength[...]

    @pl.when(o == N_OCN - 1)
    def _():
        hx_r[0] = jnp.zeros((2, L, 128), F32)

    @pl.when(o == 0)
    def _():
        hx_r[1] = jnp.zeros((2, L, 128), F32)

    @pl.when(last)
    def _():
        hy_r[0] = jnp.zeros((2, L, 256), F32)

    @pl.when(first)
    def _():
        hy_r[1] = jnp.zeros((2, L, 256), F32)

    for copy in small:
        copy.wait()
    for f in range(4):
        field = level0[f]
        surf[o, 0:32, f * 128 : (f + 1) * 128] = field[:, 0:128].astype(BF16)
        surf[o, 32:64, f * 128 : (f + 1) * 128] = field[:, 128:256].astype(BF16)
    pl.semaphore_wait(barrier, N_GRP - 1 + N_OCN - 1)

    for i in range(1, N_OCN):
        send(surf.at[o], surf.at[o], 0, lax.rem(o + i, N_OCN), g)

    @pl.when(first)
    def _():
        part = codes.at[pl.ds(0, 4)]
        over_grp(part, part, 1)

    @pl.when(last)
    def _():
        part = codes.at[pl.ds(CHUNKS - 4, 4)]
        over_grp(part, part, 1)

    @pl.when(inner)
    def _():
        part = codes.at[pl.ds(3 + g, 1)]
        over_grp(part, part, 1)

    over_grp(u_in, u_pad.at[pl.ds(1 + 8 * g, 8)], 2)

    t_copy.wait()
    lanes = lax.broadcasted_iota(jnp.int32, (L, 128), 1)
    for t in range(2):
        hy_s[0, t] = t_v[t, :, 0, :]
        hy_s[1, t] = t_v[t, :, 31, :]

        def gather(z, carry, t=t):
            west, east = carry
            tile = t_v[t, z]
            west = jnp.where(lanes == z, pltpu.roll(tile[:, 0:128], z, 1), west)
            east = jnp.where(lanes == z, pltpu.roll(tile[:, 128:256], z + 1, 1), east)
            return west, east

        zero = jnp.zeros((L, 128), F32)
        west, east = lax.fori_loop(0, L, gather, (zero, zero))
        hx_s[0, t] = west
        hx_s[1, t] = east

    def halo(src, dst, which, ocn, grp):
        return pltpu.make_async_remote_copy(
            src_ref=src,
            dst_ref=dst,
            send_sem=halo_send.at[which],
            recv_sem=halo_recv.at[which],
            device_id={"ocn": ocn, "grp": grp},
            device_id_type=MESH,
        )

    halos = (
        (o > 0, o < N_OCN - 1, halo(hx_s.at[0], hx_r.at[0], 0, jnp.maximum(o - 1, 0), g)),
        (o < N_OCN - 1, o > 0, halo(hx_s.at[1], hx_r.at[1], 1, jnp.minimum(o + 1, N_OCN - 1), g)),
        (g > 0, g < LAST, halo(hy_s.at[0], hy_r.at[0], 2, o, jnp.maximum(g - 1, 0))),
        (g < LAST, g > 0, halo(hy_s.at[1], hy_r.at[1], 3, o, jnp.minimum(g + 1, LAST))),
    )
    for sends, _, copy in halos:
        pl.when(sends)(lambda copy=copy: copy.start())

    @pl.when(polar)
    def _():
        landed(codes.at[pl.ds(0, CHUNKS - 4)], recv_sem.at[1])

    @pl.when(inner)
    def _():
        landed(codes.at[pl.ds(0, CHUNKS - 1)], recv_sem.at[1])

    code = codes[...].reshape(PADDED * 8, 128)
    here = jnp.logical_and(code >= 0, ((code >> 6) & (N_GRP - 1)) == g)
    row = ((code >> 10) << 6) + ((code & 1) << 5) + ((code & 63) >> 1)
    row = jnp.where(here, row, -1)
    lane8 = lax.broadcasted_iota(jnp.int32, (CHUNKS * 8, 128), 1)
    for part in range(4):
        hit = row[: CHUNKS * 8] == lane8 + 128 * part
        hits[part] = jnp.where(hit, 1.0, 0.0).astype(BF16)
    row_f = row.astype(F32)
    row_t = jnp.concatenate([row_f[0:128].T[0:1], row_f[128:256].T[0:1]], axis=1)
    for part in range(8):
        ids = lax.broadcasted_iota(jnp.int32, (64, 256), 0).astype(F32) + 64.0 * part
        hits_t[part * 64 : (part + 1) * 64] = jnp.where(ids == row_t, 1.0, 0.0).astype(BF16)

    landed(surf.at[pl.ds(0, N_OCN - 1)], recv_sem.at[0])
    chosen = jnp.zeros((CHUNKS * 8, 512), F32)
    for part in range(4):
        rows = surf[2 * part : 2 * part + 2].reshape(128, 512)
        chosen += jnp.dot(hits[part], rows, preferred_element_type=F32)
    sel[...] = jnp.concatenate(
        [chosen[:, f * 128 : (f + 1) * 128].reshape(CHUNKS, 8, 128) for f in range(4)], axis=1
    ).astype(BF16)
    for d in range(N_GRP):
        part = sel.at[pl.ds(chunk_of(d), chunks_of(d))]

        @pl.when(g != d)
        def _(d=d, part=part):
            send(part, slots_in.at[pl.ds(4 * g, chunks_of(d))], 3, o, d)

        @pl.when(g == d)
        def _(d=d):
            slots_in[4 * d : 4 * d + chunks_of(d)] = sel[chunk_of(d) : chunk_of(d) + chunks_of(d)]

    over_grp(mass, m_r.at[pl.ds(8 * g, 8)], 4)
    over_grp(strength, st_r.at[pl.ds(8 * g, 8)], 5)

    v_copy.wait()
    for _, arrives, copy in halos:
        pl.when(arrives)(lambda copy=copy: copy.wait_recv())
    ys = lax.broadcasted_iota(jnp.int32, (L, 256), 0)
    cols = lax.broadcasted_iota(jnp.int32, (L, 256), 1)

    def stencil(t):
        def level(z, _):
            c = t_v[t, z]
            up = jnp.where(z > 0, t_v[t, jnp.maximum(z - 1, 0)], 0.0)
            down = jnp.where(z < L - 1, t_v[t, jnp.minimum(z + 1, L - 1)], 0.0)
            he = pltpu.roll(hx_r[0, t], 127 - z, 1)
            hw = pltpu.roll(hx_r[1, t], lax.rem(128 - z, 128), 1)
            east = jnp.where(cols == 255, jnp.concatenate([he, he], axis=1), pltpu.roll(c, 255, 1))
            west = jnp.where(cols == 0, jnp.concatenate([hw, hw], axis=1), pltpu.roll(c, 1, 1))
            north = jnp.where(ys == L - 1, hy_r[0, t, pl.ds(z, 1), :], pltpu.roll(c, L - 1, 0))
            south = jnp.where(ys == 0, hy_r[1, t, pl.ds(z, 1), :], pltpu.roll(c, 1, 0))
            pre[t, z] = (
                c
                + 0.2 * (east + west + north + south - 4.0 * c)
                - 0.25 * (v_v[0, z] * (east - west) + v_v[1, z] * (north - south))
                + 0.2 * (up + down - 2.0 * c)
            )
            return 0

        lax.fori_loop(0, L, level, 0)

    stencil(0)

    w_copy.wait()

    def remap(count):
        for c in range(count):
            total = jnp.zeros((32, 128), F32)
            for s in range(N_GRP):
                total += slots_in[4 * s + c].astype(F32)
            xs[c] = total
        for r in range(4):
            out = jnp.zeros((8, 128), F32)
            for k in range(2 * count):
                x = xs[k // 2, pl.ds((k % 2) * 4 + r, 4, stride=8), :]
                x = jnp.concatenate([x, jnp.zeros((4, 128), F32)], axis=0).astype(BF16)
                out += lax.dot_general(x, w_v[r, k], (((1,), (1,)), ((), ())), preferred_element_type=F32)
            q[0, 2 * r : 2 * r + 2] = out[0:2]
            q[1, 2 * r : 2 * r + 2] = out[2:4]

    @pl.when(polar)
    def _():
        landed(slots_in.at[pl.ds(0, 4 * (N_GRP - 1))], recv_sem.at[3])
        remap(4)

    @pl.when(inner)
    def _():
        landed(slots_in.at[pl.ds(0, N_GRP - 1)], recv_sem.at[3])
        remap(1)

    tile = 8 * g + o
    m2[tile, pl.ds(0, 4, stride=2), :] = mass[o]
    m2[tile, pl.ds(1, 4, stride=2), :] = mass[o]
    base[tile] = m2[tile] * u_in[o] + wind[o] + q[1]

    def spread(i, _):
        to = lax.rem(o * N_GRP + g + i, N_ALL)
        send(base.at[tile], base.at[tile], 6, to // N_GRP, lax.rem(to, N_GRP))
        return 0

    lax.fori_loop(1, N_ALL, spread, 0)

    stencil(1)
    landed(u_pad.at[pl.ds(0, 8 * (N_GRP - 1))], recv_sem.at[2])
    landed(m_r.at[pl.ds(0, 8 * (N_GRP - 1))], recv_sem.at[4])
    landed(st_r.at[pl.ds(0, 8 * (N_GRP - 1))], recv_sem.at[5])

    def twice(i, _):
        at = pl.ds(8 * i, 8)
        m2[at, pl.ds(0, 4, stride=2), :] = m_r[at]
        m2[at, pl.ds(1, 4, stride=2), :] = m_r[at]
        st2[at, pl.ds(0, 4, stride=2), :] = st_r[at]
        st2[at, pl.ds(1, 4, stride=2), :] = st_r[at]
        return 0

    lax.fori_loop(0, N_GRP, twice, 0)
    landed(base.at[pl.ds(0, N_ALL - 1)], recv_sem.at[6])

    tiles = 4
    shape = (tiles, 8, 128)
    lane = lax.broadcasted_iota(jnp.int32, shape, 2)
    sub = lax.broadcasted_iota(jnp.int32, shape, 1)

    def dot(a, b):
        return jnp.sum(a * b, axis=0)

    def mean(acc):
        return jnp.sum(jnp.sum(acc, axis=1, keepdims=True), axis=0, keepdims=True) / (2.0 * 65536.0)

    for step in range(ITERS):

        def picard(i, sums, step=step):
            at = pl.ds(tiles * i, tiles)
            u = u_pad[pl.ds(tiles * i + 1, tiles)]
            before = u_pad[pl.ds(tiles * i, tiles)]
            after = u_pad[pl.ds(tiles * i + 2, tiles)]
            up = pltpu.roll(jnp.where(sub >= 6, before, u), 2, 1)
            down = pltpu.roll(jnp.where(sub < 2, after, u), 6, 1)
            left = pltpu.roll(jnp.where(lane == 127, up, u), 1, 2)
            right = pltpu.roll(jnp.where(lane == 0, down, u), 127, 2)
            strain = 0.5 * (right - left)
            square = strain * strain
            other = jnp.where((sub & 1) == 1, pltpu.roll(square, 1, 1), pltpu.roll(square, 7, 1))
            zeta = (0.5 * st2[at]) * lax.rsqrt(square + other + 0.25)
            new = (base[at] + zeta * (left + right)) / (m2[at] + 1.0 + 2.0 * zeta)
            res = new - u
            gval[step, at] = new
            fval[step % 2, at] = res
            if step == 0:
                return sums
            diff = res - fval[(step - 1) % 2, at]
            dval[step - 1, at] = diff
            diffs = [dval[j, at] for j in range(step - 1)] + [diff]
            terms = [dot(d, diff) for d in diffs] + [dot(d, res) for d in diffs]
            return tuple(s + t for s, t in zip(sums, terms))

        zeros = tuple(jnp.zeros((8, 128), F32) for _ in range(2 * step))
        sums = lax.fori_loop(0, N_ALL // tiles, picard, zeros)
        if step == 0:

            def first_update(i, _):
                u_pad[pl.ds(tiles * i + 1, tiles)] = gval[0, pl.ds(tiles * i, tiles)]
                return 0

            lax.fori_loop(0, N_ALL // tiles, first_update, 0)
            gram = {}
            continue
        means = [mean(s) for s in sums]
        for j in range(step):
            gram[(j, step - 1)] = means[j]
        norms = [jnp.sqrt(gram[(j, j)] + 1e-6) for j in range(step)]
        rows = [
            [
                gram[(min(a, b), max(a, b))] / (norms[a] * norms[b]) + (0.1 if a == b else 0.0)
                for b in range(step)
            ]
            + [means[step + a] / norms[a]]
            for a in range(step)
        ]
        for a in range(step):
            for b in range(a + 1, step):
                ratio = rows[b][a] / rows[a][a]
                rows[b] = [y - ratio * x for x, y in zip(rows[a], rows[b])]
        coef = [None] * step
        for a in reversed(range(step)):
            rest = rows[a][step]
            for b in range(a + 1, step):
                rest = rest - rows[a][b] * coef[b]
            coef[a] = rest / rows[a][a]
        scale = [jnp.broadcast_to(c / n, (8, 128))[None] for c, n in zip(coef, norms)]

        def combine(at, step=step, scale=scale):
            values = [gval[j, at] for j in range(step + 1)]
            out = values[step]
            for j in range(step):
                out = out - scale[j] * (values[j + 1] - values[j])
            return out

        if step < ITERS - 1:

            def update(i, _, combine=combine):
                u_pad[pl.ds(tiles * i + 1, tiles)] = combine(pl.ds(tiles * i, tiles))
                return 0

            lax.fori_loop(0, N_ALL // tiles, update, 0)
        else:
            ice[...] = combine(pl.ds(8 * g, 8))

    stress = ice[o] - q[1]
    for r in range(4):
        fx[r] = jnp.zeros((8, 128), F32)
        fx[r, 0:2] = stress[2 * r : 2 * r + 2]
        fx[r, 2:3] = 0.5 * (-0.05 * q[0, 2 * r + 1 : 2 * r + 2] - q[0, 2 * r : 2 * r + 1])

    def contribute(count):
        for r in range(4):
            x = fx[r].astype(BF16)
            for k in range(2 * count):
                out = jnp.dot(x, w_v[r, k], preferred_element_type=F32)
                cbuf[k // 2, pl.ds((k % 2) * 4 + r, 3, stride=8), :] = out[0:3]

    @pl.when(first)
    def _():
        contribute(4)
        over_grp(cbuf, crecv.at[pl.ds(0, 4)], 7)
        crecv[0:4] = cbuf[...]

    @pl.when(last)
    def _():
        contribute(4)
        over_grp(cbuf, crecv.at[pl.ds(CHUNKS - 4, 4)], 7)
        crecv[CHUNKS - 4 : CHUNKS] = cbuf[...]

    @pl.when(inner)
    def _():
        contribute(1)
        over_grp(cbuf.at[pl.ds(0, 1)], crecv.at[pl.ds(3 + g, 1)], 7)
        crecv[pl.ds(3 + g, 1)] = cbuf[0:1]

    @pl.when(polar)
    def _():
        landed(crecv.at[pl.ds(0, CHUNKS - 4)], recv_sem.at[7])

    @pl.when(inner)
    def _():
        landed(crecv.at[pl.ds(0, CHUNKS - 1)], recv_sem.at[7])

    for f in range(3):
        values = crecv[:, 8 * f : 8 * f + 8, :].reshape(PADDED * 8, 128)
        high = values.astype(BF16)
        low = (values - high.astype(F32)).astype(BF16)
        out = jnp.dot(hits_t[...], jnp.concatenate([high, low], axis=1), preferred_element_type=F32)
        out = out[:, 0:128] + out[:, 128:256]
        dense[:, f] = out.reshape(N_OCN, 64, 128)
    for i in range(1, N_OCN):
        to = lax.rem(o + i, N_OCN)
        send(dense.at[to], dense_in.at[o], 8, to, g)
    dense_in[o] = dense[o]
    landed(dense_in.at[pl.ds(0, N_OCN - 1)], recv_sem.at[8])
    for f in range(3):
        out = dense_in[0, f]
        for s in range(1, N_OCN):
            out += dense_in[s, f]
        flux[f, :, 0:128] = out[0:32]
        flux[f, :, 128:256] = out[32:64]

    landed(surf.at[pl.ds(0, N_OCN - 1)], send_sem.at[0])
    landed(u_pad.at[pl.ds(0, 8 * (N_GRP - 1))], send_sem.at[2])
    landed(m_r.at[pl.ds(0, 8 * (N_GRP - 1))], send_sem.at[4])
    landed(st_r.at[pl.ds(0, 8 * (N_GRP - 1))], send_sem.at[5])
    landed(base.at[pl.ds(0, N_ALL - 1)], send_sem.at[6])
    landed(dense_in.at[pl.ds(0, N_OCN - 1)], send_sem.at[8])

    @pl.when(polar)
    def _():
        landed(base.at[pl.ds(0, 4 * (N_GRP - 1))], send_sem.at[1])
        landed(sel.at[pl.ds(0, CHUNKS - 4)], send_sem.at[3])
        landed(gval.at[pl.ds(0, 3), pl.ds(0, 4 * (N_GRP - 1))], send_sem.at[7])

    @pl.when(inner)
    def _():
        landed(base.at[pl.ds(0, N_GRP - 1)], send_sem.at[1])
        landed(sel.at[pl.ds(0, CHUNKS - 1)], send_sem.at[3])
        landed(base.at[pl.ds(0, 3 * (N_GRP - 1))], send_sem.at[7])

    for sends, _, copy in halos:
        pl.when(sends)(lambda copy=copy: copy.wait_send())


def on_device(
    tracers,
    velocity,
    remap_weights,
    remap_blocks,
    remap_count,
    ice_velocity,
    ice_mass_rate,
    ice_strength,
    wind_stress,
):
    def tiled(x):
        return x.reshape(2, 32, 128).transpose(1, 0, 2).reshape(8, 8, 128)

    hbm = pl.BlockSpec(memory_space=pltpu.HBM)
    smem = pl.BlockSpec(memory_space=pltpu.SMEM)
    vmem = pl.BlockSpec(memory_space=pltpu.VMEM)
    scratch = [
        pltpu.VMEM((2, L, 32, 256), F32),
        pltpu.VMEM((2, L, 32, 256), F32),
        pltpu.VMEM((4, 8, 128, 128), BF16),
        pltpu.VMEM((4, 32, 256), F32),
        pltpu.VMEM((N_OCN, 64, 512), BF16),
        pltpu.VMEM((PADDED, 8, 128), jnp.int32),
        pltpu.VMEM((4, CHUNKS * 8, 128), BF16),
        pltpu.VMEM((512, 256), BF16),
        pltpu.VMEM((CHUNKS, 32, 128), BF16),
        pltpu.VMEM((4 * N_GRP, 32, 128), BF16),
        pltpu.VMEM((4, 32, 128), F32),
        pltpu.VMEM((2, 8, 128), F32),
        pltpu.VMEM((2, 2, L, 128), F32),
        pltpu.VMEM((2, 2, L, 128), F32),
        pltpu.VMEM((2, 2, L, 256), F32),
        pltpu.VMEM((2, 2, L, 256), F32),
        pltpu.VMEM((N_ALL + 2, 8, 128), F32),
        pltpu.VMEM((N_ALL, 4, 128), F32),
        pltpu.VMEM((N_ALL, 4, 128), F32),
        pltpu.VMEM((N_ALL, 8, 128), F32),
        pltpu.VMEM((N_ALL, 8, 128), F32),
        pltpu.VMEM((N_ALL, 8, 128), F32),
        pltpu.VMEM((ITERS, N_ALL, 8, 128), F32),
        pltpu.VMEM((2, N_ALL, 8, 128), F32),
        pltpu.VMEM((ITERS - 1, N_ALL, 8, 128), F32),
        pltpu.VMEM((4, 8, 128), F32),
        pltpu.VMEM((4, 24, 128), F32),
        pltpu.VMEM((PADDED, 24, 128), F32),
        pltpu.VMEM((N_OCN, 3, 64, 128), F32),
        pltpu.VMEM((N_OCN, 3, 64, 128), F32),
        pltpu.SemaphoreType.DMA((7,)),
        pltpu.SemaphoreType.DMA((9,)),
        pltpu.SemaphoreType.DMA((9,)),
        pltpu.SemaphoreType.DMA((4,)),
        pltpu.SemaphoreType.DMA((4,)),
    ]
    pre, flux, ice = pl.pallas_call(
        kernel,
        out_shape=(
            jax.ShapeDtypeStruct((2, L, 32, 256), F32),
            jax.ShapeDtypeStruct((3, 32, 256), F32),
            jax.ShapeDtypeStruct((8, 8, 128), F32),
        ),
        in_specs=[hbm, hbm, hbm, smem, smem, vmem, vmem, vmem, vmem],
        out_specs=(vmem, vmem, vmem),
        scratch_shapes=scratch,
        compiler_params=pltpu.CompilerParams(
            collective_id=0, has_side_effects=True, vmem_limit_bytes=40 * 1024 * 1024
        ),
    )(
        tracers,
        velocity,
        remap_weights,
        remap_blocks,
        remap_count,
        tiled(ice_velocity),
        tiled(wind_stress),
        ice_mass_rate.reshape(8, 4, 128),
        ice_strength.reshape(8, 4, 128),
    )
    tracers_next = pre.at[0, 0].add(0.5 * flux[2])
    ice_final = ice.reshape(32, 2, 128).transpose(1, 0, 2).reshape(2, 4096)
    return tracers_next, flux, ice_final


def solution(mesh):
    placed = (
        P(None, None, "grp", "ocn"),
        P(None, None, "grp", "ocn"),
        P("grp", None, None, None),
        P("grp", None),
        P("grp"),
        P(None, "grp"),
        P("grp"),
        P("grp"),
        P(None, "grp"),
    )
    return jax.shard_map(
        on_device,
        mesh=mesh,
        in_specs=placed,
        out_specs=(P(None, None, "grp", "ocn"), P(None, "grp", "ocn"), P(None, "grp")),
        check_vma=False,
    )
```

time: 278 us -> 89.5 us (0.32)
  the two profiles are of different devices: /device:TPU:2 before, /device:TPU:29 now
where the time goes in v1:
time: 89.5 us; the launch traced here: 89.1 us
  Pallas kernels  78.3 us (87%)
  local copies, waits for them, and re-layouts  10.1 us (11%)
    pallas_call x1, Pallas kernels, on_device(): pl.pallas_call(kernel, out_shape=(jax.ShapeDtypeStruct((2, L, 32, 256), F...  78.3 us
    unnamed x18, local copies, waits for them, and re-layouts  10.1 us

profile of v1, /device:TPU:29, one launch (start us, length us, event | category | flops | bytes accessed | tf_op | source)
XLA Modules:
  0.0 89.1 jit_solution(13386841755300359780)
XLA Ops:
  0.6 0.8 copy.14.blocks
  1.4 0.0 copy-start
  1.4 1.6 %copy-done = f32[2,32,32,256]{3,2,1,0:T(8,128)S(1)} copy-done((f32[2,32,32,256]{3,2,1,0:T(8,128)S(1)}, f32[2,32,32,256]{3,2,1,0:T(8,128)}, u32[]{:S(2)}) %copy-start) | copy-done | bytes 2097176
  3.0 0.0 copy-start.1
  3.0 1.6 %copy-done.1 = f32[2,32,32,256]{3,2,1,0:T(8,128)S(1)} copy-done((f32[2,32,32,256]{3,2,1,0:T(8,128)S(1)}, f32[2,32,32,256]{3,2,1,0:T(8,128)}, u32[]{:S(2)}) %copy-start.1) | copy-done | bytes 2097176
  4.6 0.0 copy-start.2
  4.6 0.8 copy-done.2
  5.3 0.0 copy-start.3
  5.3 0.8 copy-done.3
  6.1 0.0 copy-start.4
  6.1 0.7 copy-done.4
  6.8 0.0 copy-start.5
  6.8 0.7 copy-done.5
  7.5 0.0 copy-start.6
  7.5 0.7 copy-done.6
  8.2 78.3 %shard_map.112 = (f32[2,32,32,256]{3,2,1,0:T(8,128)S(1)}, f32[3,32,256]{2,1,0:T(8,128)S(1)}, f32[8,8,128]{2,1,0:T(8,128)S(1)}) custom-call(f32[2,32,32,256]{3,2,1,0:T(8,128)S(1)} %copy-done, f32[2,32,32,256]{3,2,1,0:T(8,128)S(1)} %copy-done.1, bf16[32,8,128,128]{3,2,1,0:T(8,128)(2,1)} %weights.1, s32[32,8]{1,0:T(8,128)S(1)} %copy.14.blocks, ...), custom_call_target="tpu_custom_call" | custom-call | tf_op jit(solution)/shard_map/pallas_call | solution.py:590
  86.5 1.3 %copy.20 = f32[2,32,32,256]{3,2,1,0:T(8,128)} copy(f32[2,32,32,256]{3,2,1,0:T(8,128)S(1)} %fusion) | data formatting | bytes 4194304
  87.8 0.6 copy.21
  88.4 0.6 copy.22
  (1 shorter events, 0.0 us)
Async XLA Ops:
  1.4 1.6 %copy-start = (f32[2,32,32,256]{3,2,1,0:T(8,128)S(1)}, f32[2,32,32,256]{3,2,1,0:T(8,128)}, u32[]{:S(2)}) copy-start(f32[2,32,32,256]{3,2,1,0:T(8,128)} %tracers.1) | copy-start | bytes 6291460
  3.0 1.6 %copy-start.1 = (f32[2,32,32,256]{3,2,1,0:T(8,128)S(1)}, f32[2,32,32,256]{3,2,1,0:T(8,128)}, u32[]{:S(2)}) copy-start(f32[2,32,32,256]{3,2,1,0:T(8,128)} %velocity.1) | copy-start | bytes 6291460
  4.6 0.8 copy-start.2
  5.3 0.8 copy-start.3
  6.1 0.7 copy-start.4
  6.8 0.7 copy-start.5
  7.5 0.7 copy-start.6

commit v2 on v1

v2 whole, which is shorter than its diff:
```python
import functools

import jax
import jax.numpy as jnp
from jax import lax
from jax.experimental import pallas as pl
from jax.experimental.pallas import tpu as pltpu
from jax.sharding import PartitionSpec as P

MESH = pl.DeviceIdType.MESH
F32 = jnp.float32
BF16 = jnp.bfloat16
N_OCN = 8
N_GRP = 16
N_ALL = N_OCN * N_GRP
LAST = N_GRP - 1
L = 32
CHUNKS = 22
PADDED = 32
ITERS = 4
TILES = 4
UNROLL = 8


def chunk_of(g):
    return 0 if g == 0 else (CHUNKS - 4 if g == LAST else 3 + g)


def chunks_of(g):
    return 4 if g in (0, LAST) else 1


def landed(ref, sem, name="left"):
    with jax.named_scope(name):
        pltpu.make_async_copy(ref, ref, sem).wait()


def kernel(
    tracers,
    velocity,
    weights,
    blocks_hbm,
    counts_hbm,
    u_hbm,
    wind_hbm,
    mass_hbm,
    strength_hbm,
    pre,
    flux,
    ice,
    blocks,
    counts,
    u_in,
    wind,
    mass,
    strength,
    t_v,
    v_v,
    w_v,
    level0,
    surf,
    codes,
    hits,
    hits_t,
    sel,
    slots_in,
    xs,
    q,
    hx_s,
    hx_r,
    hy_s,
    hy_r,
    u_r,
    u_pad,
    m_r,
    st_r,
    m2,
    st2,
    base,
    g0_pad,
    g1,
    g2,
    g3,
    f_a,
    f_b,
    d1,
    d2,
    fx,
    cbuf,
    crecv,
    dense,
    pair_in,
    dense_in,
    local_sem,
    send_sem,
    recv_sem,
    halo_send,
    halo_recv,
):
    o = lax.axis_index("ocn")
    g = lax.axis_index("grp")
    first, last = g == 0, g == LAST
    polar = jnp.logical_or(first, last)
    inner = jnp.logical_and(g > 0, g < LAST)
    z, core = o // 2, lax.rem(o, 2)
    partner = o + 1 - 2 * core
    chip = 4 * g + z

    def send(src, dst, phase, ocn, grp):
        pltpu.make_async_remote_copy(
            src_ref=src,
            dst_ref=dst,
            send_sem=send_sem.at[phase],
            recv_sem=recv_sem.at[phase],
            device_id={"ocn": ocn, "grp": grp},
            device_id_type=MESH,
        ).start()

    def over_grp(src, dst, phase):
        for i in range(1, N_GRP):
            send(src, dst, phase, o, lax.rem(g + i, N_GRP))

    small = [
        pltpu.make_async_copy(tracers.at[0, 0], level0.at[0], local_sem.at[0]),
        pltpu.make_async_copy(tracers.at[1, 0], level0.at[1], local_sem.at[1]),
        pltpu.make_async_copy(velocity.at[0, 0], level0.at[2], local_sem.at[2]),
        pltpu.make_async_copy(velocity.at[1, 0], level0.at[3], local_sem.at[3]),
    ]
    for copy in small:
        copy.start()
    index_copies = [
        pltpu.make_async_copy(blocks_hbm, blocks, local_sem.at[7]),
        pltpu.make_async_copy(counts_hbm, counts, local_sem.at[8]),
    ]
    ice_copies = [
        pltpu.make_async_copy(u_hbm, u_in, local_sem.at[9]),
        pltpu.make_async_copy(wind_hbm, wind, local_sem.at[10]),
        pltpu.make_async_copy(mass_hbm, mass, local_sem.at[11]),
        pltpu.make_async_copy(strength_hbm, strength, local_sem.at[12]),
    ]
    for copy in index_copies + ice_copies:
        copy.start()
    t_copy = pltpu.make_async_copy(tracers, t_v, local_sem.at[4])
    v_copy = pltpu.make_async_copy(velocity, v_v, local_sem.at[5])
    w_copy = pltpu.make_async_copy(weights.at[pl.ds(4 * o, 4)], w_v, local_sem.at[6])
    t_copy.start()
    w_copy.start()
    v_copy.start()

    barrier = pltpu.get_barrier_semaphore()
    for i in range(1, N_GRP):
        pl.semaphore_signal(
            barrier, inc=1, device_id={"ocn": o, "grp": lax.rem(g + i, N_GRP)}, device_id_type=MESH
        )
    for i in range(1, N_OCN):
        pl.semaphore_signal(
            barrier, inc=1, device_id={"ocn": lax.rem(o + i, N_OCN), "grp": g}, device_id_type=MESH
        )

    def fill_codes(at, count):
        for k in range(2 * count):
            for r in range(4):
                block = blocks[k, 4 * o + r]
                code = jnp.where(k < counts[4 * o + r], block, -1)
                codes[at + k // 2, pl.ds((k % 2) * 4 + r, 1), :] = jnp.full((1, 128), code, jnp.int32)

    for copy in index_copies:
        copy.wait()

    @pl.when(first)
    def _():
        fill_codes(0, 4)

    @pl.when(last)
    def _():
        fill_codes(CHUNKS - 4, 4)

    @pl.when(inner)
    def _():
        fill_codes(3 + g, 1)

    codes[pl.ds(CHUNKS, PADDED - CHUNKS)] = jnp.full((PADDED - CHUNKS, 8, 128), -1, jnp.int32)
    crecv[pl.ds(CHUNKS, PADDED - CHUNKS)] = jnp.zeros((PADDED - CHUNKS, 24, 128), F32)
    u_pad[0] = jnp.zeros((8, 128), F32)
    u_pad[N_ALL + 1] = jnp.zeros((8, 128), F32)
    for copy in ice_copies:
        copy.wait()
    g0_pad[0] = jnp.zeros((8, 128), F32)
    g0_pad[N_ALL + 1] = jnp.zeros((8, 128), F32)

    @pl.when(core == 0)
    def _():
        u_r[g, z] = u_in[z]

    @pl.when(core == 1)
    def _():
        m_r[g, z] = mass[z]
        st_r[g, z] = strength[z]


    @pl.when(o == N_OCN - 1)
    def _():
        hx_r[0] = jnp.zeros((2, L, 128), F32)

    @pl.when(o == 0)
    def _():
        hx_r[1] = jnp.zeros((2, L, 128), F32)

    @pl.when(last)
    def _():
        hy_r[0] = jnp.zeros((2, L, 256), F32)

    @pl.when(first)
    def _():
        hy_r[1] = jnp.zeros((2, L, 256), F32)

    for copy in small:
        copy.wait()
    for f in range(4):
        field = level0[f]
        surf[o, 0:32, f * 128 : (f + 1) * 128] = field[:, 0:128].astype(BF16)
        surf[o, 32:64, f * 128 : (f + 1) * 128] = field[:, 128:256].astype(BF16)
    with jax.named_scope("barrier"):
        pl.semaphore_wait(barrier, N_GRP - 1 + N_OCN - 1)

    for i in (2, 6, 3, 5, 7, 4, 1):
        send(surf.at[o], surf.at[o], 0, lax.rem(o + i, N_OCN), g)

    @pl.when(first)
    def _():
        part = codes.at[pl.ds(0, 4)]
        over_grp(part, part, 1)

    @pl.when(last)
    def _():
        part = codes.at[pl.ds(CHUNKS - 4, 4)]
        over_grp(part, part, 1)

    @pl.when(inner)
    def _():
        part = codes.at[pl.ds(3 + g, 1)]
        over_grp(part, part, 1)

    @pl.when(core == 0)
    def _():
        over_grp(u_in.at[z], u_r.at[g, z], 2)

    @pl.when(core == 1)
    def _():
        over_grp(mass.at[z], m_r.at[g, z], 2)
        over_grp(strength.at[z], st_r.at[g, z], 2)

    @pl.when(polar)
    def _():
        landed(codes.at[pl.ds(0, CHUNKS - 4)], recv_sem.at[1], "recv1")

    @pl.when(inner)
    def _():
        landed(codes.at[pl.ds(0, CHUNKS - 1)], recv_sem.at[1], "recv1")

    code = codes[...].reshape(PADDED * 8, 128)
    here = jnp.logical_and(code >= 0, ((code >> 6) & (N_GRP - 1)) == g)
    row = ((code >> 10) << 6) + ((code & 1) << 5) + ((code & 63) >> 1)
    row = jnp.where(here, row, -1)
    lane8 = lax.broadcasted_iota(jnp.int32, (CHUNKS * 8, 128), 1)
    for part in range(4):
        hit = row[: CHUNKS * 8] == lane8 + 128 * part
        hits[part] = jnp.where(hit, 1.0, 0.0).astype(BF16)
    row_f = row.astype(F32)
    row_t = jnp.concatenate([row_f[0:128].T[0:1], row_f[128:256].T[0:1]], axis=1)
    for part in range(8):
        ids = lax.broadcasted_iota(jnp.int32, (64, 256), 0).astype(F32) + 64.0 * part
        hits_t[part * 64 : (part + 1) * 64] = jnp.where(ids == row_t, 1.0, 0.0).astype(BF16)

    landed(surf.at[pl.ds(0, N_OCN - 1)], recv_sem.at[0], "recv0")
    chosen = jnp.zeros((CHUNKS * 8, 512), F32)
    for part in range(4):
        rows = surf[2 * part : 2 * part + 2].reshape(128, 512)
        chosen += jnp.dot(hits[part], rows, preferred_element_type=F32)
    sel[...] = jnp.concatenate(
        [chosen[:, f * 128 : (f + 1) * 128].reshape(CHUNKS, 8, 128) for f in range(4)], axis=1
    ).astype(BF16)
    for d in (0, LAST, *range(1, LAST)):
        for c in range(chunks_of(d)):

            @pl.when(g != d)
            def _(d=d, c=c):
                send(sel.at[chunk_of(d) + c], slots_in.at[c, g], (3, 9, 10, 12)[c], o, d)

            @pl.when(g == d)
            def _(d=d, c=c):
                slots_in[c, d] = sel[chunk_of(d) + c]

    mine = ((u_r,), (m_r, st_r))
    landed(u_r.at[pl.ds(0, N_GRP - 1), 0], recv_sem.at[2], "recv2")
    for c in range(2):

        @pl.when(core == c)
        def _(c=c):
            for i in (1, 3, 2):
                for part in mine[c]:
                    send(part.at[:, z], part.at[:, z], 4, 2 * lax.rem(z + i, 4) + core, g)

    with jax.named_scope("t_copy"):
        t_copy.wait()
    lanes = lax.broadcasted_iota(jnp.int32, (L, 128), 1)
    for t in range(2):
        hy_s[0, t] = t_v[t, :, 0, :]
        hy_s[1, t] = t_v[t, :, 31, :]

        def gather(z, carry, t=t):
            west, east = carry
            tile = t_v[t, z]
            west = jnp.where(lanes == z, pltpu.roll(tile[:, 0:128], z, 1), west)
            east = jnp.where(lanes == z, pltpu.roll(tile[:, 128:256], z + 1, 1), east)
            return west, east

        zero = jnp.zeros((L, 128), F32)
        west, east = lax.fori_loop(0, L, gather, (zero, zero), unroll=8)
        hx_s[0, t] = west
        hx_s[1, t] = east

    def halo(src, dst, which, ocn, grp):
        return pltpu.make_async_remote_copy(
            src_ref=src,
            dst_ref=dst,
            send_sem=halo_send.at[which],
            recv_sem=halo_recv.at[which],
            device_id={"ocn": ocn, "grp": grp},
            device_id_type=MESH,
        )

    halos = (
        (o > 0, o < N_OCN - 1, halo(hx_s.at[0], hx_r.at[0], 0, jnp.maximum(o - 1, 0), g)),
        (o < N_OCN - 1, o > 0, halo(hx_s.at[1], hx_r.at[1], 1, jnp.minimum(o + 1, N_OCN - 1), g)),
        (g > 0, g < LAST, halo(hy_s.at[0], hy_r.at[0], 2, o, jnp.maximum(g - 1, 0))),
        (g < LAST, g > 0, halo(hy_s.at[1], hy_r.at[1], 3, o, jnp.minimum(g + 1, LAST))),
    )
    with jax.named_scope("w_copy"):
        w_copy.wait()

    def remap(count):
        out = [jnp.zeros((8, 128), F32)] * 4
        for c in range(count):
            landed(slots_in.at[0, pl.ds(0, N_GRP - 1)], recv_sem.at[(3, 9, 10, 12)[c]], f"recv3_{c}")
            total = jnp.zeros((32, 128), F32)
            for s in range(N_GRP):
                total += slots_in[c, s].astype(F32)
            xs[c] = total
            for r in range(4):
                x = [xs[c, pl.ds(4 * k + r, 4, stride=8), :] for k in range(2)]
                x = jnp.concatenate(x, axis=1)
                x = jnp.concatenate([x, jnp.zeros(x.shape, F32)], axis=0).astype(BF16)
                w = jnp.concatenate([w_v[r, 2 * c + k] for k in range(2)], axis=1)
                out[r] += lax.dot_general(x, w, (((1,), (1,)), ((), ())), preferred_element_type=F32)
        for r in range(4):
            q[0, 2 * r : 2 * r + 2] = out[r][0:2]
            q[1, 2 * r : 2 * r + 2] = out[r][2:4]

    @pl.when(polar)
    def _():
        remap(4)

    @pl.when(inner)
    def _():
        remap(1)

    tile = 8 * g + o
    m2[tile, pl.ds(0, 4, stride=2), :] = mass[z, core]
    m2[tile, pl.ds(1, 4, stride=2), :] = mass[z, core]
    base[tile] = m2[tile] * u_in[z, core] + wind[z, core] + q[1]

    def spread(i, _):
        to = lax.rem(tile + i, N_ALL)
        send(base.at[tile], base.at[tile], 6, lax.rem(to, N_OCN), to // N_OCN)
        return 0

    lax.fori_loop(1, N_ALL, spread, 0)
    for sends, _, copy in halos:
        pl.when(sends)(lambda copy=copy: copy.start())


    landed(u_r.at[:, pl.ds(0, 3)], recv_sem.at[4], "recv4")
    for c in range(2):

        @pl.when(core == c)
        def _(c=c):
            for part in mine[c]:
                send(part, part, 5, partner, g)

    landed(u_r, recv_sem.at[5], "recv5")

    def twice(i, _):
        at = pl.ds(8 * i, 8)
        u_pad[pl.ds(8 * i + 1, 8)] = u_r[i].reshape(8, 8, 128)
        for to, part in ((m2, m_r), (st2, st_r)):
            once = part[i].reshape(8, 4, 128)
            to[at, pl.ds(0, 4, stride=2), :] = once
            to[at, pl.ds(1, 4, stride=2), :] = once
        return 0

    lax.fori_loop(0, N_GRP, twice, 0)
    landed(base.at[pl.ds(0, N_ALL - 1)], recv_sem.at[6], "recv6")

    tiles = TILES
    shape = (tiles, 8, 128)
    lane = lax.broadcasted_iota(jnp.int32, shape, 2)
    sub = lax.broadcasted_iota(jnp.int32, shape, 1)

    def dot(a, b):
        return jnp.sum(a * b, axis=0)

    def mean(acc):
        return jnp.sum(jnp.sum(acc, axis=1, keepdims=True), axis=0, keepdims=True) / (2.0 * 65536.0)

    us = (u_pad, g0_pad, u_pad, u_pad)
    fs = (f_a, f_b, f_a, None)
    ds = (None, d1, d2, None)
    gram = {}

    def g_at(k, i):
        return g0_pad[pl.ds(tiles * i + 1, tiles)] if k == 0 else (None, g1, g2, g3)[k][pl.ds(tiles * i, tiles)]

    for step in range(ITERS):

        def picard(i, sums, step=step):
            at = pl.ds(tiles * i, tiles)
            src = us[step]
            u = src[pl.ds(tiles * i + 1, tiles)]
            before = src[pl.ds(tiles * i, tiles)]
            after = src[pl.ds(tiles * i + 2, tiles)]
            up = pltpu.roll(jnp.where(sub >= 6, before, u), 2, 1)
            down = pltpu.roll(jnp.where(sub < 2, after, u), 6, 1)
            left = pltpu.roll(jnp.where(lane == 127, up, u), 1, 2)
            right = pltpu.roll(jnp.where(lane == 0, down, u), 127, 2)
            strain = 0.5 * (right - left)
            square = strain * strain
            other = jnp.where((sub & 1) == 1, pltpu.roll(square, 1, 1), pltpu.roll(square, 7, 1))
            zeta = (0.5 * st2[at]) * lax.rsqrt(square + other + 0.25)
            force = base[at]
            new = (force + zeta * (left + right)) / (m2[at] + 1.0 + 2.0 * zeta)
            res = new - u
            if step == 0:
                g0_pad[pl.ds(tiles * i + 1, tiles)] = new
                fs[0][at] = res
                return sums
            (None, g1, g2, g3)[step][at] = new
            diff = res - fs[step - 1][at]
            if step < ITERS - 1:
                fs[step][at] = res
                ds[step][at] = diff
            diffs = [ds[j][at] for j in range(1, step)] + [diff]
            terms = [dot(d, diff) for d in diffs] + [dot(d, res) for d in diffs]
            return tuple(s + t for s, t in zip(sums, terms))

        zeros = tuple(jnp.zeros((8, 128), F32) for _ in range(2 * step))
        with jax.named_scope(f"picard{step}"):
            sums = lax.fori_loop(0, N_ALL // tiles, picard, zeros, unroll=UNROLL)
        if step == 0:
            continue
        means = [mean(s) for s in sums]
        for j in range(step):
            gram[(j, step - 1)] = means[j]
        norms = [jnp.sqrt(gram[(j, j)] + 1e-6) for j in range(step)]
        rows = [
            [
                gram[(min(a, b), max(a, b))] / (norms[a] * norms[b]) + (0.1 if a == b else 0.0)
                for b in range(step)
            ]
            + [means[step + a] / norms[a]]
            for a in range(step)
        ]
        for a in range(step):
            for b in range(a + 1, step):
                ratio = rows[b][a] / rows[a][a]
                rows[b] = [y - ratio * x for x, y in zip(rows[a], rows[b])]
        coef = [None] * step
        for a in reversed(range(step)):
            rest = rows[a][step]
            for b in range(a + 1, step):
                rest = rest - rows[a][b] * coef[b]
            coef[a] = rest / rows[a][a]
        scale = [jnp.broadcast_to(c / n, (8, 128))[None] for c, n in zip(coef, norms)]

        def combine(i, step=step, scale=scale):
            values = [g_at(j, i) for j in range(step + 1)]
            out = values[step]
            for j in range(step):
                out = out - scale[j] * (values[j + 1] - values[j])
            return out

        if step < ITERS - 1:

            def update(i, _, combine=combine):
                u_pad[pl.ds(tiles * i + 1, tiles)] = combine(i)
                return 0

            with jax.named_scope(f"update{step}"):
                lax.fori_loop(0, N_ALL // tiles, update, 0, unroll=UNROLL)
        else:
            for i in range(8 // tiles):
                ice[tiles * i : tiles * (i + 1)] = combine(8 // tiles * g + i)

    stress = ice[o] - q[1]
    for r in range(4):
        fx[r] = jnp.zeros((8, 128), F32)
        fx[r, 0:2] = stress[2 * r : 2 * r + 2]
        fx[r, 2:3] = 0.5 * (-0.05 * q[0, 2 * r + 1 : 2 * r + 2] - q[0, 2 * r : 2 * r + 1])

    def contribute(count):
        for r in range(4):
            x = fx[r].astype(BF16)
            w = jnp.concatenate([w_v[r, k] for k in range(2 * count)], axis=1)
            out = jnp.dot(x, w, preferred_element_type=F32)
            for k in range(2 * count):
                cbuf[k // 2, pl.ds((k % 2) * 4 + r, 3, stride=8), :] = out[0:3, 128 * k : 128 * (k + 1)]

    @pl.when(first)
    def _():
        contribute(4)
        over_grp(cbuf, crecv.at[pl.ds(0, 4)], 7)
        crecv[0:4] = cbuf[...]

    @pl.when(last)
    def _():
        contribute(4)
        over_grp(cbuf, crecv.at[pl.ds(CHUNKS - 4, 4)], 7)
        crecv[CHUNKS - 4 : CHUNKS] = cbuf[...]

    @pl.when(inner)
    def _():
        contribute(1)
        over_grp(cbuf.at[pl.ds(0, 1)], crecv.at[pl.ds(3 + g, 1)], 7)
        crecv[pl.ds(3 + g, 1)] = cbuf[0:1]

    with jax.named_scope("v_copy"):
        v_copy.wait()
    with jax.named_scope("halos"):
        for _, arrives, copy in halos:
            pl.when(arrives)(lambda copy=copy: copy.wait_recv())
    ys = lax.broadcasted_iota(jnp.int32, (L, 256), 0)
    cols = lax.broadcasted_iota(jnp.int32, (L, 256), 1)

    def stencil(t):
        def level(z, _):
            c = t_v[t, z]
            up = jnp.where(z > 0, t_v[t, jnp.maximum(z - 1, 0)], 0.0)
            down = jnp.where(z < L - 1, t_v[t, jnp.minimum(z + 1, L - 1)], 0.0)
            he = pltpu.roll(hx_r[0, t], 127 - z, 1)
            hw = pltpu.roll(hx_r[1, t], lax.rem(128 - z, 128), 1)
            east = jnp.where(cols == 255, jnp.concatenate([he, he], axis=1), pltpu.roll(c, 255, 1))
            west = jnp.where(cols == 0, jnp.concatenate([hw, hw], axis=1), pltpu.roll(c, 1, 1))
            north = jnp.where(ys == L - 1, hy_r[0, t, pl.ds(z, 1), :], pltpu.roll(c, L - 1, 0))
            south = jnp.where(ys == 0, hy_r[1, t, pl.ds(z, 1), :], pltpu.roll(c, 1, 0))
            pre[t, z] = (
                c
                + 0.2 * (east + west + north + south - 4.0 * c)
                - 0.25 * (v_v[0, z] * (east - west) + v_v[1, z] * (north - south))
                + 0.2 * (up + down - 2.0 * c)
            )
            return 0

        lax.fori_loop(0, L, level, 0)

    with jax.named_scope("stencil0"):
        stencil(0)

    @pl.when(polar)
    def _():
        landed(crecv.at[pl.ds(0, CHUNKS - 4)], recv_sem.at[7], "recv7")

    @pl.when(inner)
    def _():
        landed(crecv.at[pl.ds(0, CHUNKS - 1)], recv_sem.at[7], "recv7")

    for f in range(3):
        values = crecv[:, 8 * f : 8 * f + 8, :].reshape(PADDED * 8, 128)
        high = values.astype(BF16)
        low = (values - high.astype(F32)).astype(BF16)
        out = jnp.dot(hits_t[...], jnp.concatenate([high, low], axis=1), preferred_element_type=F32)
        out = out[:, 0:128] + out[:, 128:256]
        out = out.reshape(4, 2, 64, 128)
        dense[0, :, f] = out[:, 0]
        dense[1, :, f] = out[:, 1]
    send(dense.at[1 - core], pair_in, 8, partner, g)
    landed(pair_in, recv_sem.at[8], "recv8")
    pair_in[...] = pair_in[...] + dense[core]
    for i in (1, 3, 2):
        to = lax.rem(z + i, 4)
        send(pair_in.at[to], dense_in.at[z], 11, 2 * to + core, g)
    dense_in[z] = pair_in[z]
    with jax.named_scope("stencil1"):
        stencil(1)
    landed(dense_in.at[pl.ds(0, 3)], recv_sem.at[11], "recv11")
    for f in range(3):
        out = dense_in[0, f] + dense_in[1, f] + dense_in[2, f] + dense_in[3, f]
        flux[f, :, 0:128] = out[0:32]
        flux[f, :, 128:256] = out[32:64]

    landed(surf.at[pl.ds(0, N_OCN - 1)], send_sem.at[0])
    landed(base.at[pl.ds(0, N_ALL - 1)], send_sem.at[6])
    landed(pair_in, send_sem.at[8])
    landed(dense_in.at[pl.ds(0, 3)], send_sem.at[11])

    landed(u_r.at[pl.ds(0, N_GRP - 1), 0], send_sem.at[2])
    landed(u_r.at[:, pl.ds(0, 3)], send_sem.at[4])
    landed(u_r, send_sem.at[5])

    @pl.when(polar)
    def _():
        landed(g1.at[pl.ds(0, 4 * (N_GRP - 1))], send_sem.at[1])
        landed(sel.at[pl.ds(0, 15)], send_sem.at[3])
        for phase in (9, 10, 12):
            landed(sel.at[0], send_sem.at[phase])
        landed(t_v.at[0, pl.ds(0, 30), 0:24], send_sem.at[7])

    @pl.when(inner)
    def _():
        landed(g1.at[pl.ds(0, N_GRP - 1)], send_sem.at[1])
        landed(sel.at[pl.ds(0, 15)], send_sem.at[3])
        for phase in (9, 10, 12):
            landed(sel.at[pl.ds(0, 2)], send_sem.at[phase])
        landed(g1.at[pl.ds(0, 3 * (N_GRP - 1))], send_sem.at[7])

    for sends, _, copy in halos:
        pl.when(sends)(lambda copy=copy: copy.wait_send())


def finish(pre, flux, ice, tracers_out, flux_out, ice_out, top, sem):
    copies = [
        pltpu.make_async_copy(pre.at[1], tracers_out.at[1], sem.at[0]),
        pltpu.make_async_copy(pre.at[0, pl.ds(1, L - 1)], tracers_out.at[0, pl.ds(1, L - 1)], sem.at[1]),
        pltpu.make_async_copy(flux, flux_out, sem.at[2]),
        pltpu.make_async_copy(ice, ice_out, sem.at[3]),
    ]
    for copy in copies:
        copy.start()
    top[...] = pre[0, 0] + 0.5 * flux[2]
    last = pltpu.make_async_copy(top, tracers_out.at[0, 0], sem.at[4])
    last.start()
    for copy in copies + [last]:
        copy.wait()


def on_device(
    tracers,
    velocity,
    remap_weights,
    remap_blocks,
    remap_count,
    ice_velocity,
    ice_mass_rate,
    ice_strength,
    wind_stress,
):
    def tiled(x):
        return x.reshape(2, 32, 128).transpose(1, 0, 2).reshape(4, 2, 8, 128)

    hbm = pl.BlockSpec(memory_space=pltpu.HBM)
    smem = pl.BlockSpec(memory_space=pltpu.SMEM)
    vmem = pl.BlockSpec(memory_space=pltpu.VMEM)
    scratch = [
        pltpu.SMEM((8, 32), jnp.int32),
        pltpu.SMEM((32,), jnp.int32),
        pltpu.VMEM((4, 2, 8, 128), F32),
        pltpu.VMEM((4, 2, 8, 128), F32),
        pltpu.VMEM((4, 2, 4, 128), F32),
        pltpu.VMEM((4, 2, 4, 128), F32),
        pltpu.VMEM((2, L, 32, 256), F32),
        pltpu.VMEM((2, L, 32, 256), F32),
        pltpu.VMEM((4, 8, 128, 128), BF16),
        pltpu.VMEM((4, 32, 256), F32),
        pltpu.VMEM((N_OCN, 64, 512), BF16),
        pltpu.VMEM((PADDED, 8, 128), jnp.int32),
        pltpu.VMEM((4, CHUNKS * 8, 128), BF16),
        pltpu.VMEM((512, 256), BF16),
        pltpu.VMEM((CHUNKS, 32, 128), BF16),
        pltpu.VMEM((4, N_GRP, 32, 128), BF16),
        pltpu.VMEM((4, 32, 128), F32),
        pltpu.VMEM((2, 8, 128), F32),
        pltpu.VMEM((2, 2, L, 128), F32),
        pltpu.VMEM((2, 2, L, 128), F32),
        pltpu.VMEM((2, 2, L, 256), F32),
        pltpu.VMEM((2, 2, L, 256), F32),
        pltpu.VMEM((N_GRP, 4, 2, 8, 128), F32),
        pltpu.VMEM((N_ALL + 2, 8, 128), F32),
        pltpu.VMEM((N_GRP, 4, 2, 4, 128), F32),
        pltpu.VMEM((N_GRP, 4, 2, 4, 128), F32),
        pltpu.VMEM((N_ALL, 8, 128), F32),
        pltpu.VMEM((N_ALL, 8, 128), F32),
        pltpu.VMEM((N_ALL, 8, 128), F32),
        pltpu.VMEM((N_ALL + 2, 8, 128), F32),
        *[pltpu.VMEM((N_ALL, 8, 128), F32)] * 7,
        pltpu.VMEM((4, 8, 128), F32),
        pltpu.VMEM((4, 24, 128), F32),
        pltpu.VMEM((PADDED, 24, 128), F32),
        pltpu.VMEM((2, 4, 3, 64, 128), F32),
        pltpu.VMEM((4, 3, 64, 128), F32),
        pltpu.VMEM((4, 3, 64, 128), F32),
        pltpu.SemaphoreType.DMA((16,)),
        pltpu.SemaphoreType.DMA((13,)),
        pltpu.SemaphoreType.DMA((13,)),
        pltpu.SemaphoreType.DMA((4,)),
        pltpu.SemaphoreType.DMA((4,)),
    ]
    pre, flux, ice = pl.pallas_call(
        kernel,
        out_shape=(
            jax.ShapeDtypeStruct((2, L, 32, 256), F32),
            jax.ShapeDtypeStruct((3, 32, 256), F32),
            jax.ShapeDtypeStruct((8, 8, 128), F32),
        ),
        in_specs=[hbm] * 9,
        out_specs=(vmem, vmem, vmem),
        scratch_shapes=scratch,
        compiler_params=pltpu.CompilerParams(
            collective_id=0, has_side_effects=True, vmem_limit_bytes=40 * 1024 * 1024
        ),
    )(
        *(
            pltpu.with_memory_space_constraint(x, pltpu.HBM)
            for x in (
                tracers,
                velocity,
                remap_weights,
                remap_blocks.T,
                remap_count,
                tiled(ice_velocity),
                tiled(wind_stress),
                ice_mass_rate.reshape(4, 2, 4, 128),
                ice_strength.reshape(4, 2, 4, 128),
            )
        )
    )
    tracers_next, flux, ice = pl.pallas_call(
        finish,
        out_shape=(
            jax.ShapeDtypeStruct((2, L, 32, 256), F32),
            jax.ShapeDtypeStruct((3, 32, 256), F32),
            jax.ShapeDtypeStruct((8, 8, 128), F32),
        ),
        in_specs=[vmem] * 3,
        out_specs=(hbm, hbm, hbm),
        scratch_shapes=[pltpu.VMEM((32, 256), F32), pltpu.SemaphoreType.DMA((5,))],
        compiler_params=pltpu.CompilerParams(vmem_limit_bytes=8 * 1024 * 1024),
    )(pre, flux, ice)
    ice_final = ice.reshape(32, 2, 128).transpose(1, 0, 2).reshape(2, 4096)
    return tracers_next, flux, ice_final


def solution(mesh):
    placed = (
        P(None, None, "grp", "ocn"),
        P(None, None, "grp", "ocn"),
        P("grp", None, None, None),
        P("grp", None),
        P("grp"),
        P(None, "grp"),
        P("grp"),
        P("grp"),
        P(None, "grp"),
    )
    return jax.shard_map(
        on_device,
        mesh=mesh,
        in_specs=placed,
        out_specs=(P(None, None, "grp", "ocn"), P(None, "grp", "ocn"), P(None, "grp")),
        check_vma=False,
    )
```

time: 89.5 us -> 56.4 us (0.63)
  the two profiles are of different devices: /device:TPU:29 before, /device:TPU:1 now
where the time goes in v2:
time: 56.4 us; the launch traced here: 55.5 us
  Pallas kernels  54.9 us (97%)
  between operations  0.64 us (1%)
    pallas_call x1, Pallas kernels, on_device(): pl.pallas_call(kernel, out_shape=(jax.ShapeDtypeStruct((2, L, 32, 256), F...  53.5 us
    pallas_call x1, Pallas kernels, on_device(): pl.pallas_call(finish, out_shape=(jax.ShapeDtypeStruct((2, L, 32, 256), F...  1.38 us

profile of v2, /device:TPU:1, one launch (start us, length us, event | category | flops | bytes accessed | tf_op | source)
XLA Modules:
  0.0 55.5 jit_solution(6631417988317431497)
XLA Ops:
  0.6 53.5 %shard_map.112 = (f32[2,32,32,256]{3,2,1,0:T(8,128)S(1)}, f32[3,32,256]{2,1,0:T(8,128)S(1)}, f32[8,8,128]{2,1,0:T(8,128)S(1)}) custom-call(f32[2,32,32,256]{3,2,1,0:T(8,128)} %tracers.1, f32[2,32,32,256]{3,2,1,0:T(8,128)} %velocity.1, bf16[32,8,128,128]{3,2,1,0:T(8,128)(2,1)} %weights.1, s32[8,32]{1,0:T(8,128)} %bitcast.22, s32[32]{0:T(128)} %counts_hbm.1, ...), custom_call_target="tpu_custom_call" | custom-call | tf_op jit(solution)/shard_map/pallas_call | solution.py:706
  54.2 1.4 %shard_map.113 = (f32[2,32,32,256]{3,2,1,0:T(8,128)}, f32[3,32,256]{2,1,0:T(8,128)}, f32[8,8,128]{2,1,0:T(8,128)}) custom-call(f32[2,32,32,256]{3,2,1,0:T(8,128)S(1)} %get-tuple-element.9.pre, f32[3,32,256]{2,1,0:T(8,128)S(1)} %get-tuple-element.10.flux, f32[8,8,128]{2,1,0:T(8,128)S(1)} %get-tuple-element.11.ice), custom_call_target="tpu_custom_call" | custom-call | tf_op jit(solution)/shard_map/pallas_call | solution.py:735

commit v3 on v2

--- a/solution.py
+++ b/solution.py
@@ -17,17 +17,45 @@
 L = 32
 CHUNKS = 22
 PADDED = 32
+PLANES_1, PLANES_4 = 4, 14
+PLANES = 2 * PLANES_4 + (N_GRP - 2) * PLANES_1
 ITERS = 4
 TILES = 4
 UNROLL = 8
 
 
+def hops(*shifts):
+    return sum(min(i, 4 - i) for i in shifts)
+
+
+FAR_GRP = sorted(range(1, N_GRP), key=lambda i: -hops(i // 4, i % 4))
+FAR_ALL = sorted(range(1, N_ALL), key=lambda i: (i * 37) % 128)
+
+
 def chunk_of(g):
     return 0 if g == 0 else (CHUNKS - 4 if g == LAST else 3 + g)
 
 
 def chunks_of(g):
     return 4 if g in (0, LAST) else 1
+
+
+def power(x):
+    return jnp.exp2(0.125 * x).astype(BF16).astype(F32)
+
+
+def eighths(x):
+    top = jnp.max(jnp.abs(x), axis=-1, keepdims=True)
+    return jnp.ceil(8.0 * jnp.log2(jnp.maximum(top * (1.0 / 32000.0), 1e-37)))
+
+
+def counted(x, step):
+    return jnp.floor(x * (1.0 / step) + 0.5).astype(jnp.int32).astype(jnp.int16)
+
+
+def halves(x):
+    high = x.astype(BF16)
+    return jnp.concatenate([high, (x - high.astype(F32)).astype(BF16)], axis=-1)
 
 
 def landed(ref, sem, name="left"):
@@ -87,10 +115,14 @@
     d2,
     fx,
     cbuf,
+    cq,
     crecv,
     dense,
     pair_in,
+    pair_q,
     dense_in,
+    pair_steps,
+    dense_steps,
     local_sem,
     send_sem,
     recv_sem,
@@ -99,12 +131,11 @@
 ):
     o = lax.axis_index("ocn")
     g = lax.axis_index("grp")
+    z, core = o // 2, lax.rem(o, 2)
+    partner = o + 1 - 2 * core
     first, last = g == 0, g == LAST
     polar = jnp.logical_or(first, last)
     inner = jnp.logical_and(g > 0, g < LAST)
-    z, core = o // 2, lax.rem(o, 2)
-    partner = o + 1 - 2 * core
-    chip = 4 * g + z
 
     def send(src, dst, phase, ocn, grp):
         pltpu.make_async_remote_copy(
@@ -116,9 +147,25 @@
             device_id_type=MESH,
         ).start()
 
+    gx, gy = g // 4, lax.rem(g, 4)
+    to_x = [lax.rem(gx + i, 4) for i in range(4)]
+    to_y = [lax.rem(gy + i, 4) for i in range(4)]
+    to_o = [2 * lax.rem(z + i, 4) + (core if c == 0 else 1 - core) for i in range(4) for c in range(2)]
+    to_g = [4 * to_x[i] + to_y[j] for i in range(4) for j in range(4)]
+
     def over_grp(src, dst, phase):
-        for i in range(1, N_GRP):
-            send(src, dst, phase, o, lax.rem(g + i, N_GRP))
+        for i in FAR_GRP:
+            send(src, dst, phase, o, to_g[i])
+
+    barrier = pltpu.get_barrier_semaphore()
+    for i in range(1, N_GRP):
+        pl.semaphore_signal(
+            barrier, inc=1, device_id={"ocn": o, "grp": lax.rem(g + i, N_GRP)}, device_id_type=MESH
+        )
+    for i in range(1, N_OCN):
+        pl.semaphore_signal(
+            barrier, inc=1, device_id={"ocn": lax.rem(o + i, N_OCN), "grp": g}, device_id_type=MESH
+        )
 
     small = [
         pltpu.make_async_copy(tracers.at[0, 0], level0.at[0], local_sem.at[0]),
@@ -147,16 +194,6 @@
     w_copy.start()
     v_copy.start()
 
-    barrier = pltpu.get_barrier_semaphore()
-    for i in range(1, N_GRP):
-        pl.semaphore_signal(
-            barrier, inc=1, device_id={"ocn": o, "grp": lax.rem(g + i, N_GRP)}, device_id_type=MESH
-        )
-    for i in range(1, N_OCN):
-        pl.semaphore_signal(
-            barrier, inc=1, device_id={"ocn": lax.rem(o + i, N_OCN), "grp": g}, device_id_type=MESH
-        )
-
     def fill_codes(at, count):
         for k in range(2 * count):
             for r in range(4):
@@ -180,7 +217,6 @@
         fill_codes(3 + g, 1)
 
     codes[pl.ds(CHUNKS, PADDED - CHUNKS)] = jnp.full((PADDED - CHUNKS, 8, 128), -1, jnp.int32)
-    crecv[pl.ds(CHUNKS, PADDED - CHUNKS)] = jnp.zeros((PADDED - CHUNKS, 24, 128), F32)
     u_pad[0] = jnp.zeros((8, 128), F32)
     u_pad[N_ALL + 1] = jnp.zeros((8, 128), F32)
     for copy in ice_copies:
@@ -370,12 +406,8 @@
     m2[tile, pl.ds(1, 4, stride=2), :] = mass[z, core]
     base[tile] = m2[tile] * u_in[z, core] + wind[z, core] + q[1]
 
-    def spread(i, _):
-        to = lax.rem(tile + i, N_ALL)
-        send(base.at[tile], base.at[tile], 6, lax.rem(to, N_OCN), to // N_OCN)
-        return 0
-
-    lax.fori_loop(1, N_ALL, spread, 0)
+    for i in FAR_ALL:
+        send(base.at[tile], base.at[tile], 6, to_o[i % 8], to_g[i // 8])
     for sends, _, copy in halos:
         pl.when(sends)(lambda copy=copy: copy.start())
 
@@ -507,31 +539,45 @@
         fx[r, 0:2] = stress[2 * r : 2 * r + 2]
         fx[r, 2:3] = 0.5 * (-0.05 * q[0, 2 * r + 1 : 2 * r + 2] - q[0, 2 * r : 2 * r + 1])
 
-    def contribute(count):
+    lane1 = lax.broadcasted_iota(jnp.int32, (8, 128), 1)
+    sub1 = lax.broadcasted_iota(jnp.int32, (8, 128), 0)
+
+    def contribute(at, count, to):
         for r in range(4):
             x = fx[r].astype(BF16)
             w = jnp.concatenate([w_v[r, k] for k in range(2 * count)], axis=1)
             out = jnp.dot(x, w, preferred_element_type=F32)
             for k in range(2 * count):
                 cbuf[k // 2, pl.ds((k % 2) * 4 + r, 3, stride=8), :] = out[0:3, 128 * k : 128 * (k + 1)]
+        table = jnp.zeros((8, 128), F32)
+        for c in range(count):
+            values = cbuf[c].reshape(3, 8, 128)
+            exponent = eighths(values)
+            cq[1 + 3 * c : 4 + 3 * c] = counted(values, power(exponent))
+            chunk = at + c
+            own = lane1 == lax.rem(chunk, 16) * 8 + sub1
+            for f in range(3):
+                line = jnp.sum(jnp.where(own, exponent[f], 0.0), axis=0, keepdims=True)
+                table += jnp.where(sub1 == 2 * f + chunk // 16, line, 0.0)
+        cq[0] = table.astype(jnp.int32).astype(jnp.int16)
+        planes = PLANES_1 if count == 1 else PLANES_4
+        if planes > 1 + 3 * count:
+            cq[planes - 1] = jnp.zeros((8, 128), jnp.int16)
+        dst = crecv.at[pl.ds(to, planes)]
+        over_grp(cq.at[pl.ds(0, planes)], dst, 7)
+        crecv[pl.ds(to, planes)] = cq[0:planes]
 
     @pl.when(first)
     def _():
-        contribute(4)
-        over_grp(cbuf, crecv.at[pl.ds(0, 4)], 7)
-        crecv[0:4] = cbuf[...]
+        contribute(0, 4, 0)
 
     @pl.when(last)
     def _():
-        contribute(4)
-        over_grp(cbuf, crecv.at[pl.ds(CHUNKS - 4, 4)], 7)
-        crecv[CHUNKS - 4 : CHUNKS] = cbuf[...]
+        contribute(CHUNKS - 4, 4, PLANES - PLANES_4)
 
     @pl.when(inner)
     def _():
-        contribute(1)
-        over_grp(cbuf.at[pl.ds(0, 1)], crecv.at[pl.ds(3 + g, 1)], 7)
-        crecv[pl.ds(3 + g, 1)] = cbuf[0:1]
+        contribute(3 + g, 1, PLANES_4 + PLANES_1 * (g - 1))
 
     with jax.named_scope("v_copy"):
         v_copy.wait()
@@ -567,33 +613,53 @@
 
     @pl.when(polar)
     def _():
-        landed(crecv.at[pl.ds(0, CHUNKS - 4)], recv_sem.at[7], "recv7")
+        landed(crecv.at[pl.ds(0, PLANES - PLANES_4)], recv_sem.at[7], "recv7")
 
     @pl.when(inner)
     def _():
-        landed(crecv.at[pl.ds(0, CHUNKS - 1)], recv_sem.at[7], "recv7")
-
+        landed(crecv.at[pl.ds(0, PLANES - PLANES_1)], recv_sem.at[7], "recv7")
+
+    starts = [0] + [PLANES_4 + PLANES_1 * i for i in range(N_GRP - 2)] + [PLANES - PLANES_4]
+    table = jnp.zeros((8, 128), F32)
+    for start in starts:
+        table += crecv[start].astype(jnp.int32).astype(F32)
+    table = power(table)
     for f in range(3):
-        values = crecv[:, 8 * f : 8 * f + 8, :].reshape(PADDED * 8, 128)
-        high = values.astype(BF16)
-        low = (values - high.astype(F32)).astype(BF16)
-        out = jnp.dot(hits_t[...], jnp.concatenate([high, low], axis=1), preferred_element_type=F32)
-        out = out[:, 0:128] + out[:, 128:256]
-        out = out.reshape(4, 2, 64, 128)
+        values = []
+        for d, start in enumerate(starts):
+            values += [crecv[start + 1 + 3 * c + f] for c in range(chunks_of(d))]
+        values = [x.astype(jnp.int32).astype(F32) for x in values]
+        values = jnp.concatenate(values + [jnp.zeros((8 * (PADDED - CHUNKS), 128), F32)], axis=0)
+        values = halves(values)
+        step = jnp.concatenate([table[2 * f : 2 * f + 1], table[2 * f + 1 : 2 * f + 2]], axis=1)
+        out = jnp.dot(hits_t[...] * step.astype(BF16), values, preferred_element_type=F32)
+        out = (out[:, 0:128] + out[:, 128:256]).reshape(4, 2, 64, 128)
         dense[0, :, f] = out[:, 0]
         dense[1, :, f] = out[:, 1]
     send(dense.at[1 - core], pair_in, 8, partner, g)
     landed(pair_in, recv_sem.at[8], "recv8")
-    pair_in[...] = pair_in[...] + dense[core]
+    lane64 = lax.broadcasted_iota(jnp.int32, (64, 128), 1)
+    row64 = lax.broadcasted_iota(jnp.int32, (64, 128), 0)
     for i in (1, 3, 2):
         to = lax.rem(z + i, 4)
-        send(pair_in.at[to], dense_in.at[z], 11, 2 * to + core, g)
-    dense_in[z] = pair_in[z]
+        total = pair_in[to] + dense[core, to]
+        step = power(eighths(total))
+        pair_q[to] = counted(total, step)
+        for f in range(3):
+            line = jnp.sum(jnp.where(lane64 == row64, step[f], 0.0), axis=0, keepdims=True)
+            pair_steps[to, f : f + 1] = line
+        send(pair_q.at[to], dense_in.at[i - 1], 11, 2 * to + core, g)
+        send(pair_steps.at[to], dense_steps.at[i - 1], 14, 2 * to + core, g)
     with jax.named_scope("stencil1"):
         stencil(1)
     landed(dense_in.at[pl.ds(0, 3)], recv_sem.at[11], "recv11")
+    landed(dense_steps.at[pl.ds(0, 3)], recv_sem.at[14], "recv14")
     for f in range(3):
-        out = dense_in[0, f] + dense_in[1, f] + dense_in[2, f] + dense_in[3, f]
+        out = pair_in[z, f] + dense[core, z, f]
+        for i in range(3):
+            step = jnp.where(lane64 == row64, dense_steps[i, f : f + 1], 0.0)
+            step = jnp.sum(step, axis=1, keepdims=True)
+            out += step * dense_in[i, f].astype(jnp.int32).astype(F32)
         flux[f, :, 0:128] = out[0:32]
         flux[f, :, 128:256] = out[32:64]
 
@@ -601,6 +667,7 @@
     landed(base.at[pl.ds(0, N_ALL - 1)], send_sem.at[6])
     landed(pair_in, send_sem.at[8])
     landed(dense_in.at[pl.ds(0, 3)], send_sem.at[11])
+    landed(dense_steps.at[pl.ds(0, 3)], send_sem.at[14])
 
     landed(u_r.at[pl.ds(0, N_GRP - 1), 0], send_sem.at[2])
     landed(u_r.at[:, pl.ds(0, 3)], send_sem.at[4])
@@ -612,7 +679,7 @@
         landed(sel.at[pl.ds(0, 15)], send_sem.at[3])
         for phase in (9, 10, 12):
             landed(sel.at[0], send_sem.at[phase])
-        landed(t_v.at[0, pl.ds(0, 30), 0:24], send_sem.at[7])
+        landed(g1.at[pl.ds(0, 7 * (N_GRP - 1))], send_sem.at[7])
 
     @pl.when(inner)
     def _():
@@ -620,7 +687,7 @@
         landed(sel.at[pl.ds(0, 15)], send_sem.at[3])
         for phase in (9, 10, 12):
             landed(sel.at[pl.ds(0, 2)], send_sem.at[phase])
-        landed(g1.at[pl.ds(0, 3 * (N_GRP - 1))], send_sem.at[7])
+        landed(crecv.at[pl.ds(0, 4 * (N_GRP - 1))], send_sem.at[7])
 
     for sends, _, copy in halos:
         pl.when(sends)(lambda copy=copy: copy.wait_send())
@@ -693,13 +760,17 @@
         *[pltpu.VMEM((N_ALL, 8, 128), F32)] * 7,
         pltpu.VMEM((4, 8, 128), F32),
         pltpu.VMEM((4, 24, 128), F32),
-        pltpu.VMEM((PADDED, 24, 128), F32),
+        pltpu.VMEM((PLANES_4, 8, 128), jnp.int16),
+        pltpu.VMEM((PLANES, 8, 128), jnp.int16),
         pltpu.VMEM((2, 4, 3, 64, 128), F32),
         pltpu.VMEM((4, 3, 64, 128), F32),
-        pltpu.VMEM((4, 3, 64, 128), F32),
+        pltpu.VMEM((4, 3, 64, 128), jnp.int16),
+        pltpu.VMEM((4, 3, 64, 128), jnp.int16),
+        pltpu.VMEM((4, 8, 128), F32),
+        pltpu.VMEM((4, 8, 128), F32),
         pltpu.SemaphoreType.DMA((16,)),
-        pltpu.SemaphoreType.DMA((13,)),
-        pltpu.SemaphoreType.DMA((13,)),
+        pltpu.SemaphoreType.DMA((15,)),
+        pltpu.SemaphoreType.DMA((15,)),
         pltpu.SemaphoreType.DMA((4,)),
         pltpu.SemaphoreType.DMA((4,)),
     ]

time: 56.4 us -> 53.1 us (0.941); the launches traced: 55.5 us -> 52.9 us
  Pallas kernels: 54.9 us -> 52.3 us
    pallas_call x1, Pallas kernels: 53.5 us -> 50.9 us  [on_device(): pl.pallas_call(kernel, out_shape=(jax.ShapeDtypeStruct((2, L, 32, 256), F...]
where the time goes in v3:
time: 53.1 us; the launch traced here: 52.9 us
  Pallas kernels  52.3 us (98%)
  between operations  0.64 us (1%)
    pallas_call x1, Pallas kernels, on_device(): pl.pallas_call(kernel, out_shape=(jax.ShapeDtypeStruct((2, L, 32, 256), F...  50.9 us
    pallas_call x1, Pallas kernels, on_device(): pl.pallas_call(finish, out_shape=(jax.ShapeDtypeStruct((2, L, 32, 256), F...  1.38 us

profile of v3, /device:TPU:1, one launch (start us, length us, event | category | flops | bytes accessed | tf_op | source)
XLA Modules:
  0.0 52.9 jit_solution(14761142799366287503)
XLA Ops:
  0.6 50.9 %shard_map.112 = (f32[2,32,32,256]{3,2,1,0:T(8,128)S(1)}, f32[3,32,256]{2,1,0:T(8,128)S(1)}, f32[8,8,128]{2,1,0:T(8,128)S(1)}) custom-call(f32[2,32,32,256]{3,2,1,0:T(8,128)} %tracers.1, f32[2,32,32,256]{3,2,1,0:T(8,128)} %velocity.1, bf16[32,8,128,128]{3,2,1,0:T(8,128)(2,1)} %weights.1, s32[8,32]{1,0:T(8,128)} %bitcast.22, s32[32]{0:T(128)} %counts_hbm.1, ...), custom_call_target="tpu_custom_call" | custom-call | tf_op jit(solution)/shard_map/pallas_call | solution.py:777
  51.6 1.4 %shard_map.113 = (f32[2,32,32,256]{3,2,1,0:T(8,128)}, f32[3,32,256]{2,1,0:T(8,128)}, f32[8,8,128]{2,1,0:T(8,128)}) custom-call(f32[2,32,32,256]{3,2,1,0:T(8,128)S(1)} %get-tuple-element.9.pre, f32[3,32,256]{2,1,0:T(8,128)S(1)} %get-tuple-element.10.flux, f32[8,8,128]{2,1,0:T(8,128)S(1)} %get-tuple-element.11.ice), custom_call_target="tpu_custom_call" | custom-call | tf_op jit(solution)/shard_map/pallas_call | solution.py:806

commit v4 on v3

--- a/solution.py
+++ b/solution.py
@@ -21,7 +21,7 @@
 PLANES = 2 * PLANES_4 + (N_GRP - 2) * PLANES_1
 ITERS = 4
 TILES = 4
-UNROLL = 8
+UNROLL = 32
 
 
 def hops(*shifts):
@@ -259,8 +259,9 @@
     with jax.named_scope("barrier"):
         pl.semaphore_wait(barrier, N_GRP - 1 + N_OCN - 1)
 
-    for i in (2, 6, 3, 5, 7, 4, 1):
-        send(surf.at[o], surf.at[o], 0, lax.rem(o + i, N_OCN), g)
+    for i in (2, 1, 3):
+        send(surf.at[o], surf.at[o], 14 + i, 2 * lax.rem(z + i, 4) + core, g)
+    send(surf.at[o], surf.at[o], 18, partner, g)
 
     @pl.when(first)
     def _():
@@ -285,6 +286,15 @@
     def _():
         over_grp(mass.at[z], m_r.at[g, z], 2)
         over_grp(strength.at[z], st_r.at[g, z], 2)
+
+    def pass_on(i):
+        part = surf.at[2 * lax.rem(z + 4 - i, 4) + core]
+        landed(part, recv_sem.at[14 + i], f"recv0_{i}")
+        send(part, part, 18 + i, partner, g)
+
+    pass_on(1)
+    pass_on(3)
+    pass_on(2)
 
     @pl.when(polar)
     def _():
@@ -308,11 +318,16 @@
         ids = lax.broadcasted_iota(jnp.int32, (64, 256), 0).astype(F32) + 64.0 * part
         hits_t[part * 64 : (part + 1) * 64] = jnp.where(ids == row_t, 1.0, 0.0).astype(BF16)
 
-    landed(surf.at[pl.ds(0, N_OCN - 1)], recv_sem.at[0], "recv0")
-    chosen = jnp.zeros((CHUNKS * 8, 512), F32)
-    for part in range(4):
-        rows = surf[2 * part : 2 * part + 2].reshape(128, 512)
-        chosen += jnp.dot(hits[part], rows, preferred_element_type=F32)
+    def select(i):
+        part = lax.rem(z + 4 - i, 4)
+        landed(surf.at[0], recv_sem.at[18 + i], f"recv18_{i}")
+        rows = surf[pl.ds(2 * part, 2)].reshape(128, 512)
+        return jnp.dot(hits[part], rows, preferred_element_type=F32)
+
+    chosen = select(0)
+    chosen += select(1)
+    chosen += select(3)
+    chosen += select(2)
     sel[...] = jnp.concatenate(
         [chosen[:, f * 128 : (f + 1) * 128].reshape(CHUNKS, 8, 128) for f in range(4)], axis=1
     ).astype(BF16)
@@ -432,7 +447,6 @@
         return 0
 
     lax.fori_loop(0, N_GRP, twice, 0)
-    landed(base.at[pl.ds(0, N_ALL - 1)], recv_sem.at[6], "recv6")
 
     tiles = TILES
     shape = (tiles, 8, 128)
@@ -453,29 +467,45 @@
     def g_at(k, i):
         return g0_pad[pl.ds(tiles * i + 1, tiles)] if k == 0 else (None, g1, g2, g3)[k][pl.ds(tiles * i, tiles)]
 
+    def drag(src, i, u):
+        at = pl.ds(tiles * i, tiles)
+        before = src[pl.ds(tiles * i, tiles)]
+        after = src[pl.ds(tiles * i + 2, tiles)]
+        up = pltpu.roll(jnp.where(sub >= 6, before, u), 2, 1)
+        down = pltpu.roll(jnp.where(sub < 2, after, u), 6, 1)
+        left = pltpu.roll(jnp.where(lane == 127, up, u), 1, 2)
+        right = pltpu.roll(jnp.where(lane == 0, down, u), 127, 2)
+        strain = 0.5 * (right - left)
+        square = strain * strain
+        other = jnp.where((sub & 1) == 1, pltpu.roll(square, 1, 1), pltpu.roll(square, 7, 1))
+        return (0.5 * st2[at]) * lax.rsqrt(square + other + 0.25), left + right
+
+    def ahead(i, _):
+        at = pl.ds(tiles * i, tiles)
+        zeta, both = drag(u_pad, i, u_pad[pl.ds(tiles * i + 1, tiles)])
+        share = 1.0 / (m2[at] + 1.0 + 2.0 * zeta)
+        d1[at] = share
+        d2[at] = zeta * both * share
+        return 0
+
+    with jax.named_scope("ahead"):
+        lax.fori_loop(0, N_ALL // tiles, ahead, 0, unroll=8)
+    landed(base.at[pl.ds(0, N_ALL - 1)], recv_sem.at[6], "recv6")
+
     for step in range(ITERS):
 
         def picard(i, sums, step=step):
             at = pl.ds(tiles * i, tiles)
             src = us[step]
             u = src[pl.ds(tiles * i + 1, tiles)]
-            before = src[pl.ds(tiles * i, tiles)]
-            after = src[pl.ds(tiles * i + 2, tiles)]
-            up = pltpu.roll(jnp.where(sub >= 6, before, u), 2, 1)
-            down = pltpu.roll(jnp.where(sub < 2, after, u), 6, 1)
-            left = pltpu.roll(jnp.where(lane == 127, up, u), 1, 2)
-            right = pltpu.roll(jnp.where(lane == 0, down, u), 127, 2)
-            strain = 0.5 * (right - left)
-            square = strain * strain
-            other = jnp.where((sub & 1) == 1, pltpu.roll(square, 1, 1), pltpu.roll(square, 7, 1))
-            zeta = (0.5 * st2[at]) * lax.rsqrt(square + other + 0.25)
-            force = base[at]
-            new = (force + zeta * (left + right)) / (m2[at] + 1.0 + 2.0 * zeta)
+            if step == 0:
+                new = base[at] * d1[at] + d2[at]
+                g0_pad[pl.ds(tiles * i + 1, tiles)] = new
+                fs[0][at] = new - u
+                return sums
+            zeta, both = drag(src, i, u)
+            new = (base[at] + zeta * both) / (m2[at] + 1.0 + 2.0 * zeta)
             res = new - u
-            if step == 0:
-                g0_pad[pl.ds(tiles * i + 1, tiles)] = new
-                fs[0][at] = res
-                return sums
             (None, g1, g2, g3)[step][at] = new
             diff = res - fs[step - 1][at]
             if step < ITERS - 1:
@@ -663,7 +693,8 @@
         flux[f, :, 0:128] = out[0:32]
         flux[f, :, 128:256] = out[32:64]
 
-    landed(surf.at[pl.ds(0, N_OCN - 1)], send_sem.at[0])
+    for phase in (15, 16, 17, 18, 19, 20, 21):
+        landed(surf.at[0], send_sem.at[phase])
     landed(base.at[pl.ds(0, N_ALL - 1)], send_sem.at[6])
     landed(pair_in, send_sem.at[8])
     landed(dense_in.at[pl.ds(0, 3)], send_sem.at[11])
@@ -769,8 +800,8 @@
         pltpu.VMEM((4, 8, 128), F32),
         pltpu.VMEM((4, 8, 128), F32),
         pltpu.SemaphoreType.DMA((16,)),
-        pltpu.SemaphoreType.DMA((15,)),
-        pltpu.SemaphoreType.DMA((15,)),
+        pltpu.SemaphoreType.DMA((22,)),
+        pltpu.SemaphoreType.DMA((22,)),
         pltpu.SemaphoreType.DMA((4,)),
         pltpu.SemaphoreType.DMA((4,)),
     ]

time: 53.1 us -> 50.2 us (0.945)
  Pallas kernels: 52.3 us -> 49.5 us
    pallas_call x1, Pallas kernels: 50.9 us -> 48.1 us  [on_device(): pl.pallas_call(kernel, out_shape=(jax.ShapeDtypeStruct((2, L, 32, 256), F...]
where the time goes in v4:
time: 50.2 us; the launch traced here: 50.1 us
  Pallas kernels  49.5 us (99%)
  between operations  0.64 us (1%)
    pallas_call x1, Pallas kernels, on_device(): pl.pallas_call(kernel, out_shape=(jax.ShapeDtypeStruct((2, L, 32, 256), F...  48.1 us
    pallas_call x1, Pallas kernels, on_device(): pl.pallas_call(finish, out_shape=(jax.ShapeDtypeStruct((2, L, 32, 256), F...  1.38 us

profile of v4, /device:TPU:1, one launch (start us, length us, event | category | flops | bytes accessed | tf_op | source)
XLA Modules:
  0.0 50.1 jit_solution(17034742560307737097)
XLA Ops:
  0.6 48.1 %shard_map.112 = (f32[2,32,32,256]{3,2,1,0:T(8,128)S(1)}, f32[3,32,256]{2,1,0:T(8,128)S(1)}, f32[8,8,128]{2,1,0:T(8,128)S(1)}) custom-call(f32[2,32,32,256]{3,2,1,0:T(8,128)} %tracers.1, f32[2,32,32,256]{3,2,1,0:T(8,128)} %velocity.1, bf16[32,8,128,128]{3,2,1,0:T(8,128)(2,1)} %weights.1, s32[8,32]{1,0:T(8,128)} %bitcast.22, s32[32]{0:T(128)} %counts_hbm.1, ...), custom_call_target="tpu_custom_call" | custom-call | tf_op jit(solution)/shard_map/pallas_call | solution.py:808
  48.7 1.4 %shard_map.113 = (f32[2,32,32,256]{3,2,1,0:T(8,128)}, f32[3,32,256]{2,1,0:T(8,128)}, f32[8,8,128]{2,1,0:T(8,128)}) custom-call(f32[2,32,32,256]{3,2,1,0:T(8,128)S(1)} %get-tuple-element.9.pre, f32[3,32,256]{2,1,0:T(8,128)S(1)} %get-tuple-element.10.flux, f32[8,8,128]{2,1,0:T(8,128)S(1)} %get-tuple-element.11.ice), custom_call_target="tpu_custom_call" | custom-call | tf_op jit(solution)/shard_map/pallas_call | solution.py:837

commit v5 on v4

--- a/solution.py
+++ b/solution.py
@@ -29,7 +29,9 @@
 
 
 FAR_GRP = sorted(range(1, N_GRP), key=lambda i: -hops(i // 4, i % 4))
-FAR_ALL = sorted(range(1, N_ALL), key=lambda i: (i * 37) % 128)
+FAR_ALL = sorted(range(1, N_ALL), key=lambda i: (-hops(i // 32, i // 8 % 4, i // 2 % 4) // 2, (i * 37) % 128))
+HELPERS = {(0, 2): 1, (0, 3): 4, (LAST, 2): LAST - 1, (LAST, 3): LAST - 4}
+FAR_FIRST = sorted(range(1, N_ALL), key=lambda i: -hops(i // 32, i // 8 % 4, i // 2 % 4))
 
 
 def chunk_of(g):
@@ -92,6 +94,9 @@
     hits_t,
     sel,
     slots_in,
+    help_in,
+    help_out,
+    helped,
     xs,
     q,
     hx_s,
@@ -318,6 +323,16 @@
         ids = lax.broadcasted_iota(jnp.int32, (64, 256), 0).astype(F32) + 64.0 * part
         hits_t[part * 64 : (part + 1) * 64] = jnp.where(ids == row_t, 1.0, 0.0).astype(BF16)
 
+    mine = ((u_r,), (m_r, st_r))
+    landed(u_r.at[pl.ds(0, N_GRP - 1), 0], recv_sem.at[2], "recv2")
+    for c in range(2):
+
+        @pl.when(core == c)
+        def _(c=c):
+            for i in (1, 3, 2):
+                for part in mine[c]:
+                    send(part.at[:, z], part.at[:, z], 4, 2 * lax.rem(z + i, 4) + core, g)
+
     def select(i):
         part = lax.rem(z + 4 - i, 4)
         landed(surf.at[0], recv_sem.at[18 + i], f"recv18_{i}")
@@ -331,26 +346,22 @@
     sel[...] = jnp.concatenate(
         [chosen[:, f * 128 : (f + 1) * 128].reshape(CHUNKS, 8, 128) for f in range(4)], axis=1
     ).astype(BF16)
-    for d in (0, LAST, *range(1, LAST)):
-        for c in range(chunks_of(d)):
-
-            @pl.when(g != d)
-            def _(d=d, c=c):
-                send(sel.at[chunk_of(d) + c], slots_in.at[c, g], (3, 9, 10, 12)[c], o, d)
-
-            @pl.when(g == d)
-            def _(d=d, c=c):
-                slots_in[c, d] = sel[chunk_of(d) + c]
-
-    mine = ((u_r,), (m_r, st_r))
-    landed(u_r.at[pl.ds(0, N_GRP - 1), 0], recv_sem.at[2], "recv2")
+    def give(at, dst, own, phase, d):
+        @pl.when(g != d)
+        def _():
+            send(sel.at[at], dst.at[g], phase, o, d)
+
+        @pl.when(g == d)
+        def _():
+            own[d] = sel[at]
+
+    for (d, c), helper in HELPERS.items():
+        give(chunk_of(d) + c, help_in, help_in, 10, helper)
     for c in range(2):
-
-        @pl.when(core == c)
-        def _(c=c):
-            for i in (1, 3, 2):
-                for part in mine[c]:
-                    send(part.at[:, z], part.at[:, z], 4, 2 * lax.rem(z + i, 4) + core, g)
+        for d in (0, LAST):
+            give(chunk_of(d) + c, slots_in.at[c], slots_in.at[c], (3, 9)[c], d)
+    for d in range(1, LAST):
+        give(chunk_of(d), slots_in.at[0], slots_in.at[0], 3, d)
 
     with jax.named_scope("t_copy"):
         t_copy.wait()
@@ -387,17 +398,33 @@
         (g > 0, g < LAST, halo(hy_s.at[0], hy_r.at[0], 2, o, jnp.maximum(g - 1, 0))),
         (g < LAST, g > 0, halo(hy_s.at[1], hy_r.at[1], 3, o, jnp.minimum(g + 1, LAST))),
     )
+    def collected(part):
+        total = jnp.zeros((32, 128), F32)
+        for s in range(N_GRP):
+            total += part[s].astype(F32)
+        return total
+
+    for (d, c), helper in HELPERS.items():
+
+        @pl.when(g == helper)
+        def _(d=d, c=c):
+            landed(help_in.at[pl.ds(0, N_GRP - 1)], recv_sem.at[10], "recv10")
+            help_out[...] = collected(help_in).astype(BF16)
+            send(help_out, helped.at[c - 2], 12, o, d)
+
     with jax.named_scope("w_copy"):
         w_copy.wait()
 
     def remap(count):
         out = [jnp.zeros((8, 128), F32)] * 4
         for c in range(count):
-            landed(slots_in.at[0, pl.ds(0, N_GRP - 1)], recv_sem.at[(3, 9, 10, 12)[c]], f"recv3_{c}")
-            total = jnp.zeros((32, 128), F32)
-            for s in range(N_GRP):
-                total += slots_in[c, s].astype(F32)
-            xs[c] = total
+            if c < 2:
+                landed(slots_in.at[0, pl.ds(0, N_GRP - 1)], recv_sem.at[(3, 9)[c]], f"recv3_{c}")
+                xs[c] = collected(slots_in.at[c])
+            else:
+                if c == 2:
+                    landed(helped, recv_sem.at[12], "recv3_3")
+                xs[c] = helped[c - 2].astype(F32)
             for r in range(4):
                 x = [xs[c, pl.ds(4 * k + r, 4, stride=8), :] for k in range(2)]
                 x = jnp.concatenate(x, axis=1)
@@ -421,8 +448,12 @@
     m2[tile, pl.ds(1, 4, stride=2), :] = mass[z, core]
     base[tile] = m2[tile] * u_in[z, core] + wind[z, core] + q[1]
 
-    for i in FAR_ALL:
-        send(base.at[tile], base.at[tile], 6, to_o[i % 8], to_g[i // 8])
+    def spread(order):
+        for i in order:
+            send(base.at[tile], base.at[tile], 6, to_o[i % 8], to_g[i // 8])
+
+    pl.when(polar)(lambda: spread(FAR_FIRST))
+    pl.when(inner)(lambda: spread(FAR_ALL))
     for sends, _, copy in halos:
         pl.when(sends)(lambda copy=copy: copy.start())
 
@@ -708,17 +739,27 @@
     def _():
         landed(g1.at[pl.ds(0, 4 * (N_GRP - 1))], send_sem.at[1])
         landed(sel.at[pl.ds(0, 15)], send_sem.at[3])
-        for phase in (9, 10, 12):
-            landed(sel.at[0], send_sem.at[phase])
+        landed(sel.at[0], send_sem.at[9])
+        landed(sel.at[pl.ds(0, 4)], send_sem.at[10])
         landed(g1.at[pl.ds(0, 7 * (N_GRP - 1))], send_sem.at[7])
 
     @pl.when(inner)
     def _():
         landed(g1.at[pl.ds(0, N_GRP - 1)], send_sem.at[1])
         landed(sel.at[pl.ds(0, 15)], send_sem.at[3])
-        for phase in (9, 10, 12):
-            landed(sel.at[pl.ds(0, 2)], send_sem.at[phase])
+        landed(sel.at[pl.ds(0, 2)], send_sem.at[9])
         landed(crecv.at[pl.ds(0, 4 * (N_GRP - 1))], send_sem.at[7])
+
+    helps = functools.reduce(jnp.logical_or, [g == d for d in HELPERS.values()])
+
+    @pl.when(helps)
+    def _():
+        landed(sel.at[pl.ds(0, 3)], send_sem.at[10])
+        landed(sel.at[0], send_sem.at[12])
+
+    @pl.when(jnp.logical_and(inner, jnp.logical_not(helps)))
+    def _():
+        landed(sel.at[pl.ds(0, 4)], send_sem.at[10])
 
     for sends, _, copy in halos:
         pl.when(sends)(lambda copy=copy: copy.wait_send())
@@ -773,7 +814,10 @@
         pltpu.VMEM((4, CHUNKS * 8, 128), BF16),
         pltpu.VMEM((512, 256), BF16),
         pltpu.VMEM((CHUNKS, 32, 128), BF16),
-        pltpu.VMEM((4, N_GRP, 32, 128), BF16),
+        pltpu.VMEM((2, N_GRP, 32, 128), BF16),
+        pltpu.VMEM((N_GRP, 32, 128), BF16),
+        pltpu.VMEM((32, 128), BF16),
+        pltpu.VMEM((2, 32, 128), BF16),
         pltpu.VMEM((4, 32, 128), F32),
         pltpu.VMEM((2, 8, 128), F32),
         pltpu.VMEM((2, 2, L, 128), F32),

time: 50.2 us -> 48.5 us (0.966)
  Pallas kernels: 49.5 us -> 47.7 us
    pallas_call x1, Pallas kernels: 48.1 us -> 46.3 us  [on_device(): pl.pallas_call(kernel, out_shape=(jax.ShapeDtypeStruct((2, L, 32, 256), F...]
where the time goes in v5:
time: 48.5 us; the launch traced here: 48.4 us
  Pallas kernels  47.7 us (98%)
  between operations  0.64 us (1%)
    pallas_call x1, Pallas kernels, on_device(): pl.pallas_call(kernel, out_shape=(jax.ShapeDtypeStruct((2, L, 32, 256), F...  46.3 us
    pallas_call x1, Pallas kernels, on_device(): pl.pallas_call(finish, out_shape=(jax.ShapeDtypeStruct((2, L, 32, 256), F...  1.38 us

profile of v5, /device:TPU:1, one launch (start us, length us, event | category | flops | bytes accessed | tf_op | source)
XLA Modules:
  0.0 48.4 jit_solution(1581847204785352061)
XLA Ops:
  0.6 46.3 %shard_map.112 = (f32[2,32,32,256]{3,2,1,0:T(8,128)S(1)}, f32[3,32,256]{2,1,0:T(8,128)S(1)}, f32[8,8,128]{2,1,0:T(8,128)S(1)}) custom-call(f32[2,32,32,256]{3,2,1,0:T(8,128)} %tracers.1, f32[2,32,32,256]{3,2,1,0:T(8,128)} %velocity.1, bf16[32,8,128,128]{3,2,1,0:T(8,128)(2,1)} %weights.1, s32[8,32]{1,0:T(8,128)} %bitcast.22, s32[32]{0:T(128)} %counts_hbm.1, ...), custom_call_target="tpu_custom_call" | custom-call | tf_op jit(solution)/shard_map/pallas_call | solution.py:852
  47.0 1.4 %shard_map.113 = (f32[2,32,32,256]{3,2,1,0:T(8,128)}, f32[3,32,256]{2,1,0:T(8,128)}, f32[8,8,128]{2,1,0:T(8,128)}) custom-call(f32[2,32,32,256]{3,2,1,0:T(8,128)S(1)} %get-tuple-element.9.pre, f32[3,32,256]{2,1,0:T(8,128)S(1)} %get-tuple-element.10.flux, f32[8,8,128]{2,1,0:T(8,128)S(1)} %get-tuple-element.11.ice), custom_call_target="tpu_custom_call" | custom-call | tf_op jit(solution)/shard_map/pallas_call | solution.py:881

commit v6 on v5

--- a/solution.py
+++ b/solution.py
@@ -356,7 +356,17 @@
             own[d] = sel[at]
 
     for (d, c), helper in HELPERS.items():
-        give(chunk_of(d) + c, help_in, help_in, 10, helper)
+        at = chunk_of(d) + c
+        alone = jnp.logical_and(g == helper, core == 1)
+
+        @pl.when(jnp.logical_not(alone))
+        def _(at=at, helper=helper):
+            send(sel.at[at], help_in.at[core, g], 22 + core, 2 * z + 1, helper)
+
+        @pl.when(alone)
+        def _(at=at, helper=helper):
+            help_in[1, helper] = sel[at]
+
     for c in range(2):
         for d in (0, LAST):
             give(chunk_of(d) + c, slots_in.at[c], slots_in.at[c], (3, 9)[c], d)
@@ -406,11 +416,14 @@
 
     for (d, c), helper in HELPERS.items():
 
-        @pl.when(g == helper)
+        @pl.when(jnp.logical_and(g == helper, core == 1))
         def _(d=d, c=c):
-            landed(help_in.at[pl.ds(0, N_GRP - 1)], recv_sem.at[10], "recv10")
-            help_out[...] = collected(help_in).astype(BF16)
-            send(help_out, helped.at[c - 2], 12, o, d)
+            landed(help_in.at[1, pl.ds(0, N_GRP - 1)], recv_sem.at[23], "recv23")
+            help_out[1] = collected(help_in.at[1]).astype(BF16)
+            send(help_out.at[1], helped.at[c - 2], 12, 2 * z + 1, d)
+            landed(help_in.at[0], recv_sem.at[22], "recv22")
+            help_out[0] = collected(help_in.at[0]).astype(BF16)
+            send(help_out.at[0], helped.at[c - 2], 10, 2 * z, d)
 
     with jax.named_scope("w_copy"):
         w_copy.wait()
@@ -423,7 +436,7 @@
                 xs[c] = collected(slots_in.at[c])
             else:
                 if c == 2:
-                    landed(helped, recv_sem.at[12], "recv3_3")
+                    landed(helped, recv_sem.at[10 + 2 * core], "recv3_3")
                 xs[c] = helped[c - 2].astype(F32)
             for r in range(4):
                 x = [xs[c, pl.ds(4 * k + r, 4, stride=8), :] for k in range(2)]
@@ -446,11 +459,13 @@
     tile = 8 * g + o
     m2[tile, pl.ds(0, 4, stride=2), :] = mass[z, core]
     m2[tile, pl.ds(1, 4, stride=2), :] = mass[z, core]
-    base[tile] = m2[tile] * u_in[z, core] + wind[z, core] + q[1]
+    chip = 4 * g + z
+    base[chip, core] = m2[tile] * u_in[z, core] + wind[z, core] + q[1]
 
     def spread(order):
         for i in order:
-            send(base.at[tile], base.at[tile], 6, to_o[i % 8], to_g[i // 8])
+            if i % 2 == 0:
+                send(base.at[chip, core], base.at[chip, core], 6, to_o[i % 8], to_g[i // 8])
 
     pl.when(polar)(lambda: spread(FAR_FIRST))
     pl.when(inner)(lambda: spread(FAR_ALL))
@@ -497,6 +512,9 @@
 
     def g_at(k, i):
         return g0_pad[pl.ds(tiles * i + 1, tiles)] if k == 0 else (None, g1, g2, g3)[k][pl.ds(tiles * i, tiles)]
+
+    def force(i):
+        return base[pl.ds(tiles // 2 * i, tiles // 2)].reshape(shape)
 
     def drag(src, i, u):
         at = pl.ds(tiles * i, tiles)
@@ -521,7 +539,9 @@
 
     with jax.named_scope("ahead"):
         lax.fori_loop(0, N_ALL // tiles, ahead, 0, unroll=8)
-    landed(base.at[pl.ds(0, N_ALL - 1)], recv_sem.at[6], "recv6")
+    landed(base.at[pl.ds(0, N_ALL // 2 - 1), 0], recv_sem.at[6], "recv6")
+    send(base.at[:, core], base.at[:, core], 13, partner, g)
+    landed(base.at[:, 0], recv_sem.at[13], "recv13")
 
     for step in range(ITERS):
 
@@ -530,12 +550,12 @@
             src = us[step]
             u = src[pl.ds(tiles * i + 1, tiles)]
             if step == 0:
-                new = base[at] * d1[at] + d2[at]
+                new = force(i) * d1[at] + d2[at]
                 g0_pad[pl.ds(tiles * i + 1, tiles)] = new
                 fs[0][at] = new - u
                 return sums
             zeta, both = drag(src, i, u)
-            new = (base[at] + zeta * both) / (m2[at] + 1.0 + 2.0 * zeta)
+            new = (force(i) + zeta * both) / (m2[at] + 1.0 + 2.0 * zeta)
             res = new - u
             (None, g1, g2, g3)[step][at] = new
             diff = res - fs[step - 1][at]
@@ -726,7 +746,8 @@
 
     for phase in (15, 16, 17, 18, 19, 20, 21):
         landed(surf.at[0], send_sem.at[phase])
-    landed(base.at[pl.ds(0, N_ALL - 1)], send_sem.at[6])
+    landed(base.at[pl.ds(0, N_ALL // 2 - 1), 0], send_sem.at[6])
+    landed(base.at[:, 0], send_sem.at[13])
     landed(pair_in, send_sem.at[8])
     landed(dense_in.at[pl.ds(0, 3)], send_sem.at[11])
     landed(dense_steps.at[pl.ds(0, 3)], send_sem.at[14])
@@ -740,7 +761,6 @@
         landed(g1.at[pl.ds(0, 4 * (N_GRP - 1))], send_sem.at[1])
         landed(sel.at[pl.ds(0, 15)], send_sem.at[3])
         landed(sel.at[0], send_sem.at[9])
-        landed(sel.at[pl.ds(0, 4)], send_sem.at[10])
         landed(g1.at[pl.ds(0, 7 * (N_GRP - 1))], send_sem.at[7])
 
     @pl.when(inner)
@@ -752,14 +772,17 @@
 
     helps = functools.reduce(jnp.logical_or, [g == d for d in HELPERS.values()])
 
+    helps = jnp.logical_and(helps, core == 1)
+
     @pl.when(helps)
     def _():
-        landed(sel.at[pl.ds(0, 3)], send_sem.at[10])
+        landed(sel.at[pl.ds(0, 3)], send_sem.at[23])
+        landed(sel.at[0], send_sem.at[10])
         landed(sel.at[0], send_sem.at[12])
 
-    @pl.when(jnp.logical_and(inner, jnp.logical_not(helps)))
-    def _():
-        landed(sel.at[pl.ds(0, 4)], send_sem.at[10])
+    @pl.when(jnp.logical_not(helps))
+    def _():
+        landed(sel.at[pl.ds(0, 4)], send_sem.at[22 + core])
 
     for sends, _, copy in halos:
         pl.when(sends)(lambda copy=copy: copy.wait_send())
@@ -815,8 +838,8 @@
         pltpu.VMEM((512, 256), BF16),
         pltpu.VMEM((CHUNKS, 32, 128), BF16),
         pltpu.VMEM((2, N_GRP, 32, 128), BF16),
-        pltpu.VMEM((N_GRP, 32, 128), BF16),
-        pltpu.VMEM((32, 128), BF16),
+        pltpu.VMEM((2, N_GRP, 32, 128), BF16),
+        pltpu.VMEM((2, 32, 128), BF16),
         pltpu.VMEM((2, 32, 128), BF16),
         pltpu.VMEM((4, 32, 128), F32),
         pltpu.VMEM((2, 8, 128), F32),
@@ -830,7 +853,7 @@
         pltpu.VMEM((N_GRP, 4, 2, 4, 128), F32),
         pltpu.VMEM((N_ALL, 8, 128), F32),
         pltpu.VMEM((N_ALL, 8, 128), F32),
-        pltpu.VMEM((N_ALL, 8, 128), F32),
+        pltpu.VMEM((N_ALL // 2, 2, 8, 128), F32),
         pltpu.VMEM((N_ALL + 2, 8, 128), F32),
         *[pltpu.VMEM((N_ALL, 8, 128), F32)] * 7,
         pltpu.VMEM((4, 8, 128), F32),
@@ -844,8 +867,8 @@
         pltpu.VMEM((4, 8, 128), F32),
         pltpu.VMEM((4, 8, 128), F32),
         pltpu.SemaphoreType.DMA((16,)),
-        pltpu.SemaphoreType.DMA((22,)),
-        pltpu.SemaphoreType.DMA((22,)),
+        pltpu.SemaphoreType.DMA((24,)),
+        pltpu.SemaphoreType.DMA((24,)),
         pltpu.SemaphoreType.DMA((4,)),
         pltpu.SemaphoreType.DMA((4,)),
     ]

time: 48.5 us -> 46.5 us (0.959)
  Pallas kernels: 47.7 us -> 45.3 us
    pallas_call x1, Pallas kernels: 46.3 us -> 43.9 us  [on_device(): pl.pallas_call(kernel, out_shape=(jax.ShapeDtypeStruct((2, L, 32, 256), F...]
where the time goes in v6:
time: 46.5 us; the launch traced here: 45.9 us
  Pallas kernels  45.3 us (97%)
  between operations  0.64 us (1%)
    pallas_call x1, Pallas kernels, on_device(): pl.pallas_call(kernel, out_shape=(jax.ShapeDtypeStruct((2, L, 32, 256), F...  43.9 us
    pallas_call x1, Pallas kernels, on_device(): pl.pallas_call(finish, out_shape=(jax.ShapeDtypeStruct((2, L, 32, 256), F...  1.38 us

profile of v6, /device:TPU:1, one launch (start us, length us, event | category | flops | bytes accessed | tf_op | source)
XLA Modules:
  0.0 45.9 jit_solution(9387177917081406967)
XLA Ops:
  0.6 43.9 %shard_map.112 = (f32[2,32,32,256]{3,2,1,0:T(8,128)S(1)}, f32[3,32,256]{2,1,0:T(8,128)S(1)}, f32[8,8,128]{2,1,0:T(8,128)S(1)}) custom-call(f32[2,32,32,256]{3,2,1,0:T(8,128)} %tracers.1, f32[2,32,32,256]{3,2,1,0:T(8,128)} %velocity.1, bf16[32,8,128,128]{3,2,1,0:T(8,128)(2,1)} %weights.1, s32[8,32]{1,0:T(8,128)} %bitcast.22, s32[32]{0:T(128)} %counts_hbm.1, ...), custom_call_target="tpu_custom_call" | custom-call | tf_op jit(solution)/shard_map/pallas_call | solution.py:875
  44.5 1.4 %shard_map.113 = (f32[2,32,32,256]{3,2,1,0:T(8,128)}, f32[3,32,256]{2,1,0:T(8,128)}, f32[8,8,128]{2,1,0:T(8,128)}) custom-call(f32[2,32,32,256]{3,2,1,0:T(8,128)S(1)} %get-tuple-element.9.pre, f32[3,32,256]{2,1,0:T(8,128)S(1)} %get-tuple-element.10.flux, f32[8,8,128]{2,1,0:T(8,128)S(1)} %get-tuple-element.11.ice), custom_call_target="tpu_custom_call" | custom-call | tf_op jit(solution)/shard_map/pallas_call | solution.py:904

commit v7 on v6

--- a/solution.py
+++ b/solution.py
@@ -717,12 +717,15 @@
         out = (out[:, 0:128] + out[:, 128:256]).reshape(4, 2, 64, 128)
         dense[0, :, f] = out[:, 0]
         dense[1, :, f] = out[:, 1]
-    send(dense.at[1 - core], pair_in, 8, partner, g)
-    landed(pair_in, recv_sem.at[8], "recv8")
+    pair_phase = {2: 8, 1: 0, 3: 24, 0: 25}
+    for i, phase in pair_phase.items():
+        to = lax.rem(z + i, 4)
+        send(dense.at[1 - core, to], pair_in.at[to], phase, partner, g)
     lane64 = lax.broadcasted_iota(jnp.int32, (64, 128), 1)
     row64 = lax.broadcasted_iota(jnp.int32, (64, 128), 0)
-    for i in (1, 3, 2):
+    for i in (2, 1, 3):
         to = lax.rem(z + i, 4)
+        landed(pair_in.at[to], recv_sem.at[pair_phase[i]], "recv8")
         total = pair_in[to] + dense[core, to]
         step = power(eighths(total))
         pair_q[to] = counted(total, step)
@@ -733,6 +736,7 @@
         send(pair_steps.at[to], dense_steps.at[i - 1], 14, 2 * to + core, g)
     with jax.named_scope("stencil1"):
         stencil(1)
+    landed(pair_in.at[z], recv_sem.at[25], "recv25")
     landed(dense_in.at[pl.ds(0, 3)], recv_sem.at[11], "recv11")
     landed(dense_steps.at[pl.ds(0, 3)], recv_sem.at[14], "recv14")
     for f in range(3):
@@ -748,7 +752,8 @@
         landed(surf.at[0], send_sem.at[phase])
     landed(base.at[pl.ds(0, N_ALL // 2 - 1), 0], send_sem.at[6])
     landed(base.at[:, 0], send_sem.at[13])
-    landed(pair_in, send_sem.at[8])
+    for phase in pair_phase.values():
+        landed(pair_in.at[0], send_sem.at[phase])
     landed(dense_in.at[pl.ds(0, 3)], send_sem.at[11])
     landed(dense_steps.at[pl.ds(0, 3)], send_sem.at[14])
 
@@ -867,8 +872,8 @@
         pltpu.VMEM((4, 8, 128), F32),
         pltpu.VMEM((4, 8, 128), F32),
         pltpu.SemaphoreType.DMA((16,)),
-        pltpu.SemaphoreType.DMA((24,)),
-        pltpu.SemaphoreType.DMA((24,)),
+        pltpu.SemaphoreType.DMA((26,)),
+        pltpu.SemaphoreType.DMA((26,)),
         pltpu.SemaphoreType.DMA((4,)),
         pltpu.SemaphoreType.DMA((4,)),
     ]

time: 46.5 us -> 46.1 us (level)
  no operation moved by 1% of the time
where the time goes in v7:
time: 46.1 us; the launch traced here: 45.6 us
  Pallas kernels  44.9 us (97%)
  between operations  0.64 us (1%)
    pallas_call x1, Pallas kernels, on_device(): pl.pallas_call(kernel, out_shape=(jax.ShapeDtypeStruct((2, L, 32, 256), F...  43.5 us
    pallas_call x1, Pallas kernels, on_device(): pl.pallas_call(finish, out_shape=(jax.ShapeDtypeStruct((2, L, 32, 256), F...  1.38 us

profile of v7, /device:TPU:1, one launch (start us, length us, event | category | flops | bytes accessed | tf_op | source)
XLA Modules:
  0.0 45.6 jit_solution(14659536149471345957)
XLA Ops:
  0.6 43.5 %shard_map.112 = (f32[2,32,32,256]{3,2,1,0:T(8,128)S(1)}, f32[3,32,256]{2,1,0:T(8,128)S(1)}, f32[8,8,128]{2,1,0:T(8,128)S(1)}) custom-call(f32[2,32,32,256]{3,2,1,0:T(8,128)} %tracers.1, f32[2,32,32,256]{3,2,1,0:T(8,128)} %velocity.1, bf16[32,8,128,128]{3,2,1,0:T(8,128)(2,1)} %weights.1, s32[8,32]{1,0:T(8,128)} %bitcast.22, s32[32]{0:T(128)} %counts_hbm.1, ...), custom_call_target="tpu_custom_call" | custom-call | tf_op jit(solution)/shard_map/pallas_call | solution.py:880
  44.2 1.4 %shard_map.113 = (f32[2,32,32,256]{3,2,1,0:T(8,128)}, f32[3,32,256]{2,1,0:T(8,128)}, f32[8,8,128]{2,1,0:T(8,128)}) custom-call(f32[2,32,32,256]{3,2,1,0:T(8,128)S(1)} %get-tuple-element.9.pre, f32[3,32,256]{2,1,0:T(8,128)S(1)} %get-tuple-element.10.flux, f32[8,8,128]{2,1,0:T(8,128)S(1)} %get-tuple-element.11.ice), custom_call_target="tpu_custom_call" | custom-call | tf_op jit(solution)/shard_map/pallas_call | solution.py:909
